TPU v7x, 16 devices: a 4x2x1 block of a 4x4x8 slice. The times are simulated.
16 devices in a mesh: dp: 2 (over y, z), tp: 8 (over x, core).
Axes of the slice: x: 4, y: 2, z: 1, core: 2. Of those that a mesh axis runs over, the one named last changes fastest.
The devices are a block of a 4x4x8 slice.
Arguments:
- k_cache: bfloat16 [8, 32, 4096, 128], P('dp', None, 'tp'), parts along dimension 0
- v_cache: bfloat16 [8, 32, 4096, 128], P('dp', None, 'tp'), parts along dimension 0
- prompt_len: int32 [8], P('dp'), parts along dimension 0
- x_steps: bfloat16 [64, 8, 4096], P(None, 'dp'), parts along dimension 1
- w_norm: bfloat16 [4096], replicated
- w_q: bfloat16 [4096, 4096], P(None, 'tp')
- w_k: bfloat16 [4096, 4096], P(None, 'tp')
- w_v: bfloat16 [4096, 4096], P(None, 'tp')
- w_o: bfloat16 [4096, 4096], P('tp')
Outputs:
- output 1: bfloat16 [64, 8, 4096], P(None, 'dp'), parts along dimension 1
- output 2: bfloat16 [8, 32, 4160, 128], P('dp', 'tp'), parts along dimension 0
- output 3: bfloat16 [8, 32, 4160, 128], P('dp', 'tp'), parts along dimension 0
There are 2 independent parts. A program takes and returns all parts, laid end to end along the dimension named above; an argument that names none is the same for every part.
All inputs are finite; a program needn't handle non-finite values.
Results may differ from a plain program's by a relative error of at most 0.0174102.
Values are sent between devices in bfloat16 or wider.
A program may use at most 768 MiB of HBM per device.

v0:
```python
import jax
import jax.numpy as jnp
from jax import lax
from jax.sharding import PartitionSpec as P

ROPE_BASE = 10000.0
NORM_EPS = 1e-6


def rotate(values, positions):
    half_dim = values.shape[-1] // 2
    inv_freq = ROPE_BASE ** (-2.0 * jnp.arange(half_dim, dtype=jnp.float32) / values.shape[-1])
    angles = positions.astype(jnp.float32)[..., None] * inv_freq
    cos_part = jnp.cos(angles)
    sin_part = jnp.sin(angles)
    first_half = values[..., :half_dim]
    second_half = values[..., half_dim:]
    return jnp.concatenate([first_half * cos_part - second_half * sin_part, second_half * cos_part + first_half * sin_part], axis=-1)


def write_row(cache_row, new_row, start_slot):
    return lax.dynamic_update_slice(cache_row, new_row, (0, start_slot, 0))


def decode_heads(k_heads, v_heads, prompt_len, residual, w_norm, w_q, w_k, w_v, w_o):
    num_steps, num_rows, model_dim = residual.shape
    head_dim = k_heads.shape[-1]
    seq_len = k_heads.shape[2]
    num_heads = w_q.shape[1] // head_dim
    inv_rms = lax.rsqrt(jnp.mean(residual * residual, axis=-1, keepdims=True) + NORM_EPS)
    normed = (residual * inv_rms * (1.0 + w_norm.astype(jnp.float32))).astype(jnp.bfloat16)
    positions = (prompt_len[:, None] + jnp.arange(num_steps)[None, :])[:, None, :]

    def project(weight):
        return jnp.einsum("udo,ojf->djuf", normed, weight.reshape(model_dim, num_heads, head_dim), preferred_element_type=jnp.float32).astype(jnp.bfloat16)

    queries = (rotate(project(w_q).astype(jnp.float32), positions) * head_dim ** -0.5).astype(jnp.bfloat16)
    key_new = rotate(project(w_k).astype(jnp.float32), positions).astype(jnp.bfloat16)
    val_new = project(w_v)
    old_scores = jnp.einsum("bhsd,bhtd->bhst", queries, k_heads, preferred_element_type=jnp.float32)
    new_scores = jnp.einsum("bhsd,bhrd->bhsr", queries, key_new, preferred_element_type=jnp.float32)
    old_valid = (jnp.arange(seq_len)[None, :] < prompt_len[:, None])[:, None, None, :]
    new_valid = jnp.arange(num_steps)[None, :] <= jnp.arange(num_steps)[:, None]
    old_scores = jnp.where(old_valid, old_scores, -jnp.inf)
    new_scores = jnp.where(new_valid, new_scores, -jnp.inf)
    row_peak = jnp.maximum(jnp.max(old_scores, axis=-1, keepdims=True), jnp.max(new_scores, axis=-1, keepdims=True))
    old_exp = jnp.exp(old_scores - row_peak)
    new_exp = jnp.exp(new_scores - row_peak)
    norm_sum = jnp.sum(old_exp, axis=-1, keepdims=True) + jnp.sum(new_exp, axis=-1, keepdims=True)
    heads_out = jnp.einsum("bhst,bhtd->bhsd", (old_exp / norm_sum).astype(jnp.bfloat16), v_heads, preferred_element_type=jnp.float32)
    heads_out = heads_out + jnp.einsum("bhsr,bhrd->bhsd", (new_exp / norm_sum).astype(jnp.bfloat16), val_new, preferred_element_type=jnp.float32)
    attn_part = jnp.einsum("bhsd,hdm->sbm", heads_out.astype(jnp.bfloat16), w_o.reshape(num_heads, head_dim, model_dim), preferred_element_type=jnp.float32)
    zero_tail = jnp.zeros((num_rows, num_heads, num_steps, head_dim), jnp.bfloat16)
    k_out = jax.vmap(write_row)(jnp.concatenate([k_heads, zero_tail], axis=2), key_new, prompt_len)
    v_out = jax.vmap(write_row)(jnp.concatenate([v_heads, zero_tail], axis=2), val_new, prompt_len)
    return attn_part, k_out, v_out


def solution(mesh):
    def local_block(k_cache, v_cache, prompt_len, x_steps, w_norm, w_q, w_k, w_v, w_o):
        k_heads = lax.all_to_all(k_cache, "tp", 1, 2, tiled=True)
        v_heads = lax.all_to_all(v_cache, "tp", 1, 2, tiled=True)
        residual = x_steps.astype(jnp.float32)
        attn_part, k_out, v_out = decode_heads(k_heads, v_heads, prompt_len, residual, w_norm, w_q, w_k, w_v, w_o)
        attn_sum = lax.psum(attn_part.astype(jnp.bfloat16), "tp")
        y_steps = (residual + attn_sum.astype(jnp.float32)).astype(jnp.bfloat16)
        return y_steps, k_out, v_out

    cache_spec = P("dp", None, "tp", None)
    col_spec = P(None, "tp")
    out_cache_spec = P("dp", "tp", None, None)
    return jax.shard_map(local_block, mesh=mesh, in_specs=(cache_spec, cache_spec, P("dp"), P(None, "dp", None), P(None), col_spec, col_spec, col_spec, P("tp", None)), out_specs=(P(None, "dp", None), out_cache_spec, out_cache_spec), check_vma=False)
```

profile of v0, /device:TPU:113, one launch (start us, length us, event | category | flops | bytes accessed | tf_op | source)
XLA Modules:
  0.0 539.6 jit_solution(7754512507161683601)
XLA Ops:
  7.2 14.0 %copy.23 = bf16[4,32,512,128]{3,2,0,1:T(8,128)(2,1)} copy(bf16[4,32,512,128]{3,2,1,0:T(8,128)(2,1)} %param.9) | data formatting | bytes 33554432 | tf_op args[0]
  21.2 6.4 %all-to-all-start = ((bf16[4,32,512,128]{3,2,0,1:T(8,128)(2,1)}), bf16[4,32,512,128]{3,2,0,1:T(8,128)(2,1)}, u32[]{:S(2)}, u32[]{:S(2)}) async-start(bf16[4,32,512,128]{3,2,0,1:T(8,128)(2,1)} %copy.23), calls=%async_computation | async-start | bytes 33554432 | tf_op jit(solution)/shard_map/all_to_all | solution.py:61
  27.6 14.0 %copy.26 = bf16[4,32,512,128]{3,2,0,1:T(8,128)(2,1)} copy(bf16[4,32,512,128]{3,2,1,0:T(8,128)(2,1)} %param.10) | data formatting | bytes 33554432 | tf_op args[1]
  41.6 169.3 %all-to-all-done = bf16[4,32,512,128]{3,2,0,1:T(8,128)(2,1)} async-done(((bf16[4,32,512,128]{3,2,0,1:T(8,128)(2,1)}), bf16[4,32,512,128]{3,2,0,1:T(8,128)(2,1)}, u32[]{:S(2)}, u32[]{:S(2)}) %all-to-all-start) | async-done | bytes 16777248 | tf_op jit(solution)/shard_map/all_to_all | solution.py:61
  210.9 7.0 %all-to-all-start.1 = ((bf16[4,32,512,128]{3,2,0,1:T(8,128)(2,1)}), bf16[4,32,512,128]{3,2,0,1:T(8,128)(2,1)}, u32[]{:S(2)}, u32[]{:S(2)}) async-start(bf16[4,32,512,128]{3,2,0,1:T(8,128)(2,1)} %copy.26), calls=%async_computation.1 | async-start | bytes 33554432 | tf_op jit(solution)/shard_map/all_to_all | solution.py:62
  221.1 4.3 fusion.19
  231.7 14.2 %copy.24 = bf16[4,8,4,512,128]{4,3,1,2,0:T(8,128)(2,1)} copy(bf16[4,8,4,512,128]{4,3,0,2,1:T(8,128)(2,1)} %bitcast.4) | data formatting | bytes 33554432 | tf_op jit(solution)/shard_map/all_to_all | solution.py:61
  245.9 12.7 %select_reduce_fusion = (f32[4,4,64]{2,1,0:T(4,128)S(1)}, f32[4,4,64,4096]{3,2,1,0:T(8,128)}) fusion(pred[4,4096]{1,0:T(4,128)(4,1)S(1)} %iota_compare_fusion, bf16[4,4,64,128]{3,2,1,0:T(8,128)(2,1)S(1)} %fusion.26, bf16[4,4,4096,128]{3,2,1,0:T(8,128)(2,1)} %bitcast.140), kind=kOutput, calls=%fused_computation.8 | convolution fusion | flops 1082129408 | bytes 33837056 | tf_op jit(solution)/shard_map/bhsd,bhtd->bhst/dot_general | solution.py:40
  258.7 9.1 %fusion = f32[4,4,64]{2,1,0:T(4,128)S(1)} fusion(f32[4,4,64,4096]{3,2,1,0:T(8,128)} %get-tuple-element.74, f32[4,4,64]{2,1,0:T(4,128)S(1)} %max.8, pred[4,4096]{1,0:T(4,128)(4,1)S(1)} %iota_compare_fusion), kind=kLoop, calls=%fused_computation.9 | loop fusion | flops 12581888 | bytes 16801792 | tf_op jit(solution)/shard_map/reduce_sum | solution.py:49
  267.9 133.6 %all-to-all-done.1 = bf16[4,32,512,128]{3,2,0,1:T(8,128)(2,1)} async-done(((bf16[4,32,512,128]{3,2,0,1:T(8,128)(2,1)}), bf16[4,32,512,128]{3,2,0,1:T(8,128)(2,1)}, u32[]{:S(2)}, u32[]{:S(2)}) %all-to-all-start.1) | async-done | bytes 16777248 | tf_op jit(solution)/shard_map/all_to_all | solution.py:62
  401.4 8.3 %copy.27 = bf16[4,4,8,512,128]{4,3,2,1,0:T(8,128)(2,1)S(1)} copy(bf16[4,4,8,512,128]{4,3,0,1,2:T(8,128)(2,1)} %bitcast.11) | data formatting | bytes 33554432 | tf_op jit(solution)/shard_map/all_to_all | solution.py:62
  409.7 19.0 %concatenate.19 = bf16[4,4,4160,128]{3,2,1,0:T(8,128)(2,1)} pad(bf16[4,4,4096,128]{3,2,1,0:T(8,128)(2,1)} %bitcast.141, bf16[]{:T(256)} %constant.8.clone.1), padding=0_0x0_0x0_64x0_0 | pad | bytes 33816576 | tf_op jit(solution)/shard_map/concatenate | solution.py:54
  428.8 6.6 %concatenate.21 = bf16[4,4,4160,128]{3,2,1,0:T(8,128)(2,1)} pad(bf16[4,4,4096,128]{3,2,1,0:T(8,128)(2,1)S(1)} %bitcast.142, bf16[]{:T(256)} %constant.8.clone.1), padding=0_0x0_0x0_64x0_0 | pad | bytes 33816576 | tf_op jit(solution)/shard_map/concatenate | solution.py:55
  436.4 15.8 %fusion.4 = bf16[64,4,4096]{2,0,1:T(8,128)(2,1)} fusion(bf16[4,128,4096,1]{2,1,0,3:T(8,128)(2,1)} %bitcast.144, f32[4,4,64,128]{3,2,1,0:T(8,128)} %fusion.28, bf16[4,4,4096,128]{3,2,1,0:T(8,128)(2,1)} %bitcast.143, f32[4,4,64,4096]{3,2,1,0:T(8,128)} %get-tuple-element.74, f32[4,4,64]{2,1,0:T(4,128)S(1)} %add.74, f32[4,4,64]{2,1,0:T(4,128)S(1)} %max.8, ...), kind=kOutput, calls=%fused_computation.17 | convolution fusion | flops 2165571584 | bytes 40394752 | tf_op jit(solution)/shard_map/bhsd,hdm->sbm/dot_general | solution.py:52
  452.3 37.3 %while.2 = (s32[]{:T(128)}, bf16[4,4,4160,128]{3,2,1,0:T(8,128)(2,1)}, s32[4,4]{1,0:T(4,128)S(1)}, bf16[4,4,64,128]{3,2,1,0:T(8,128)(2,1)S(1)}, s32[]{:T(128)}, /*index=5*/s32[4]{0:T(128)S(1)}, s32[]{:T(128)}) while((s32[]{:T(128)}, bf16[4,4,4160,128]{3,2,1,0:T(8,128)(2,1)}, s32[4,4]{1,0:T(4,128)S(1)}, bf16[4,4,64,128]{3,2,1,0:T(8,128)(2,1)S(1)}, ...), condition=%wide.while_cond, body=%wide.while_body.sunk | while | flops 32797 | bytes 327875 | solution.py:22
  453.0 3.1 and_reduce_fusion.4
  458.9 2.8 dynamic-update-slice.6
  462.3 3.1 and_reduce_fusion.4
  468.2 2.8 dynamic-update-slice.6
  471.7 3.1 and_reduce_fusion.4
  477.6 2.8 dynamic-update-slice.6
  481.0 3.1 and_reduce_fusion.4
  489.6 37.3 %while.3 = (s32[]{:T(128)}, bf16[4,4,4160,128]{3,2,1,0:T(8,128)(2,1)}, s32[4,4]{1,0:T(4,128)S(1)}, bf16[4,4,64,128]{3,2,1,0:T(8,128)(2,1)S(1)}, s32[]{:T(128)}, /*index=5*/s32[4]{0:T(128)S(1)}, s32[]{:T(128)}) while((s32[]{:T(128)}, bf16[4,4,4160,128]{3,2,1,0:T(8,128)(2,1)}, s32[4,4]{1,0:T(4,128)S(1)}, bf16[4,4,64,128]{3,2,1,0:T(8,128)(2,1)S(1)}, ...), condition=%wide.while_cond.1, body=%wide.while_body.1.sunk | while | flops 32797 | bytes 327875 | solution.py:22
  490.3 3.1 and_reduce_fusion.5
  496.2 2.8 dynamic-update-slice.7
  499.6 3.1 and_reduce_fusion.5
  505.5 2.8 dynamic-update-slice.7
  509.0 3.1 and_reduce_fusion.5
  514.9 2.8 dynamic-update-slice.7
  518.3 3.1 and_reduce_fusion.5
  526.9 2.9 fusion.8
  529.8 2.9 copy.31
  (69 shorter events, 43.2 us)
Async XLA Ops:
  21.2 189.7 %all-to-all-start = ((bf16[4,32,512,128]{3,2,0,1:T(8,128)(2,1)}), bf16[4,32,512,128]{3,2,0,1:T(8,128)(2,1)}, u32[]{:S(2)}, u32[]{:S(2)}) async-start(bf16[4,32,512,128]{3,2,0,1:T(8,128)(2,1)} %copy.23), calls=%async_computation | async-start | bytes 33554432 | tf_op jit(solution)/shard_map/all_to_all | solution.py:61
  41.6 176.4 %copy-start.4 = (s32[4]{0:T(128)S(1)}, s32[4]{0:T(128)}, u32[]{:S(2)}) copy-start(s32[4]{0:T(128)} %param.11) | copy-start | bytes 52
  41.6 176.4 %copy-start.5 = (s32[3]{0:T(128)S(1)}, s32[3]{0:T(128)}, u32[]{:S(2)}) copy-start(s32[3]{0:T(128)} %constant.11.clone.1) | copy-start | bytes 40
  41.6 176.7 %copy-start.1 = (bf16[64,4,4096]{2,1,0:T(4,128)(2,1)S(1)}, bf16[64,4,4096]{2,1,0:T(4,128)(2,1)}, u32[]{:S(2)}) copy-start(bf16[64,4,4096]{2,1,0:T(4,128)(2,1)} %param.12) | copy-start | bytes 6291460
  41.6 179.0 %copy-start.3 = (bf16[4096]{0:T(1024)(128)(2,1)S(1)}, bf16[4096]{0:T(1024)(128)(2,1)}, u32[]{:S(2)}) copy-start(bf16[4096]{0:T(1024)(128)(2,1)} %param.13) | copy-start | bytes 24580
  210.9 190.5 %all-to-all-start.1 = ((bf16[4,32,512,128]{3,2,0,1:T(8,128)(2,1)}), bf16[4,32,512,128]{3,2,0,1:T(8,128)(2,1)}, u32[]{:S(2)}, u32[]{:S(2)}) async-start(bf16[4,32,512,128]{3,2,0,1:T(8,128)(2,1)} %copy.26), calls=%async_computation.1 | async-start | bytes 33554432 | tf_op jit(solution)/shard_map/all_to_all | solution.py:62
  217.9 309.0 %all-reduce.4.cloned.1.call-start = ((), (), s32[]{:S(2)}) async-start(), calls=%async_computation.2 | async-start | bytes 4194304 | tf_op jit(solution)/shard_map/psum | solution.py:65
  221.1 4.3 copy-start.6
  227.4 2.2 copy-start.7
  409.7 19.1 %copy-start = (bf16[4,4,8,512,128]{4,3,2,1,0:T(8,128)(2,1)}, bf16[4,4,8,512,128]{4,3,2,1,0:T(8,128)(2,1)S(1)}, u32[]{:S(2)}) copy-start(bf16[4,4,8,512,128]{4,3,2,1,0:T(8,128)(2,1)S(1)} %copy.27) | copy-start | bytes 50331652
  436.4 15.9 %copy-start.2 = (s32[4]{0:T(128)S(1)}, s32[4]{0:T(128)}, u32[]{:S(2)}) copy-start(s32[4]{0:T(128)} %constant.114) | copy-start | bytes 52
Sparse Core Ops, SparseCore 0:
  452.4 56.4 all-reduce.3
where the time goes:
time: 542 us; the launch traced here: 540 us
  waiting for transfers between devices  303 us (56%)
  local copies, waits for them, and re-layouts  108 us (20%)
  other arithmetic  63.2 us (12%)
  matrix products  38.2 us (7%)
  between operations  14.2 us (3%)
  starting transfers between devices  13.4 us (2%)
    all_to_all x1, waiting for transfers between devices, local_block(): k_heads = lax.all_to_all(k_cache, 'tp', 1, 2, tiled=True)  169 us
    all_to_all x1, waiting for transfers between devices, local_block(): v_heads = lax.all_to_all(v_cache, 'tp', 1, 2, tiled=True)  134 us
    scatter x16, other arithmetic  47.2 us
    unnamed x21, local copies, waits for them, and re-layouts  32.2 us
    scatter x24, local copies, waits for them, and re-layouts  27.3 us
    concatenate x1, local copies, waits for them, and re-layouts, decode_heads(): jnp.concatenate([k_heads, zero_tail], axis=2)  19 us
    dot_general x1, matrix products, decode_heads(): jnp.einsum('bhsd,hdm->sbm', heads_out.astype(jnp.bfloat16), w_o.reshape(n...  15.8 us
    all_to_all x1, local copies, waits for them, and re-layouts, local_block(): k_heads = lax.all_to_all(k_cache, 'tp', 1, 2, tiled=True)  14.2 us
  transfers between devices with their start and end apart: 3, of which 2 were waited for; matrix products, arithmetic and copies ran while one was open for 25% of the time, Pallas kernels for 0%

commit v1 on v0

v1 whole, which is shorter than its diff:
```python
import functools

import jax
import jax.numpy as jnp
from jax import lax
from jax.experimental import pallas as pl
from jax.experimental.pallas import tpu as pltpu
from jax.sharding import PartitionSpec as P

ROPE_BASE = 10000.0
NORM_EPS = 1e-6
CORES = 2
WINDOW_ALIGN = 16
MESH = pl.DeviceIdType.MESH
F32 = jnp.float32
BF16 = jnp.bfloat16
ANY = pl.BlockSpec(memory_space=pl.ANY)
VMEM = pl.BlockSpec(memory_space=pltpu.VMEM)
SMEM = pl.BlockSpec(memory_space=pltpu.SMEM)


def dot(a, b):
    return lax.dot_general(a, b, (((1,), (0,)), ((), ())), preferred_element_type=F32)


def dot_t(a, b):
    return lax.dot_general(a, b, (((1,), (1,)), ((), ())), preferred_element_type=F32)


def exchange_kernel(
    chips, steps, plen_ref, k_ref, v_ref, x_ref, gain_ref, wq_ref, wk_ref, wv_ref, wo_ref, cos_ref, sin_ref,
    kf, vf, kn, vn, yf,
    stage, xs, gs, cs, sn, hs, wb, wo_own, wo_peer, qs, sc, pb, pn, o_own, o_peer, yp, rs,
    kv_send, kv_recv, kv_own, w_sem, in_sem, wo_sems, o_send, o_recv, rs_send, rs_recv, ag_send, ag_recv, d_send, d_recv,
):
    rows, heads, _, head_dim = kn.shape
    out_len = kf.shape[2]
    shard = k_ref.shape[2]
    seq_len = out_len - steps
    parts = chips * CORES
    model = wq_ref.shape[0]
    width = heads * head_dim
    half = model // CORES
    block = half // chips
    group = lax.axis_index("dp")
    me = lax.axis_index("tp")
    chip, core = me // CORES, lax.rem(me, CORES)
    partner = chip * CORES + (1 - core)

    hops = [(1, 0), (chips - 1, 0)] + [(d, 0) for d in range(2, chips - 1)]
    hops += [(1, 1), (chips - 1, 1)] + [(d, 1) for d in range(2, chips - 1)] + [(0, 1)]

    def peer(hop):
        return lax.rem(chip + hop[0], chips) * CORES + lax.rem(core + hop[1], CORES)

    def remote(src, dst, send, recv, target):
        return pltpu.make_async_remote_copy(src_ref=src, dst_ref=dst, send_sem=send, recv_sem=recv, device_id=(group, target), device_id_type=MESH)

    barrier = pltpu.get_barrier_semaphore()
    for hop in hops:
        pl.semaphore_signal(barrier, inc=1, device_id=(group, peer(hop)), device_id_type=MESH)
    pl.semaphore_wait(barrier, parts - 1)

    slots = pl.ds(pl.multiple_of(me * shard, shard), shard)

    def cache_copy(kind, b, n):
        src, dst = ((k_ref, kf), (v_ref, vf))[kind]
        target = peer(hops[n])
        return remote(src.at[b, pl.ds(target * heads, heads)], dst.at[b, :, slots, :], kv_send.at[kind, b, n], kv_recv.at[kind, b, n], target)

    def own_copy(kind, b):
        src, dst = ((k_ref, kf), (v_ref, vf))[kind]
        return pltpu.make_async_copy(src.at[b, pl.ds(me * heads, heads)], dst.at[b, :, slots, :], kv_own.at[kind, b])

    def half_cols(which):
        return pl.ds(pl.multiple_of(which * half, half), half)

    wo_send = remote(wo_ref.at[:, half_cols(1 - core)], wo_peer, wo_sems.at[0], wo_sems.at[1], partner)
    wo_send.start()
    for b in range(rows):
        for kind in range(2):
            for n in range(len(hops)):
                cache_copy(kind, b, n).start()

    loads = [
        pltpu.make_async_copy(gain_ref, gs, in_sem.at[0]),
        pltpu.make_async_copy(cos_ref, cs, in_sem.at[1]),
        pltpu.make_async_copy(sin_ref, sn, in_sem.at[2]),
        pltpu.make_async_copy(wo_ref.at[:, half_cols(core)], wo_own, in_sem.at[3]),
    ]
    for c in loads:
        c.start()
    pair = wb.shape[2]
    groups = width // pair
    w_loads = [
        pltpu.make_async_copy((wq_ref, wk_ref, wv_ref)[i // groups].at[:, i % groups * pair:(i % groups + 1) * pair], wb.at[i % 2], w_sem.at[i])
        for i in range(3 * groups)
    ]
    w_loads[0].start()
    w_loads[1].start()
    for b in range(rows):
        for kind in range(2):
            own_copy(kind, b).start()
    zero_tail = jnp.zeros((rows, heads, steps, head_dim), BF16)
    kf[:, :, seq_len:, :] = zero_tail
    vf[:, :, seq_len:, :] = zero_tail
    for c in loads:
        c.wait()

    gain = 1.0 + gs[...].astype(F32)
    part_steps = stage.shape[0]
    for t in range(0, steps, part_steps):
        x_load = pltpu.make_async_copy(x_ref.at[t:t + part_steps], stage, in_sem.at[4])
        x_load.start()
        x_load.wait()
        for b in range(rows):
            x = stage[:, b, :]
            xs[b, t:t + part_steps, :] = x
            residual = x.astype(F32)
            inv_rms = lax.rsqrt(jnp.mean(residual * residual, axis=-1, keepdims=True) + NORM_EPS)
            hs[b * steps + t:b * steps + t + part_steps, :] = (residual * inv_rms * gain).astype(BF16)

    for i, load in enumerate(w_loads):
        load.wait()
        matrix, j = i // groups, i % groups
        flat = dot(hs[...], wb[i % 2]).astype(BF16)
        if i + 2 < len(w_loads):
            w_loads[i + 2].start()
        for sub in range(pair // head_dim):
            for b in range(rows):
                u = flat[b * steps:(b + 1) * steps, sub * head_dim:(sub + 1) * head_dim]
                if matrix < 2:
                    u = u.astype(F32)
                    u = u * cs[b] + pltpu.roll(u, head_dim // 2, 1) * sn[b]
                    if matrix == 0:
                        u = u * head_dim ** -0.5
                (qs, kn, vn)[matrix][b, j * (pair // head_dim) + sub] = u.astype(BF16)

    wo_send.wait()
    causal = lax.broadcasted_iota(jnp.int32, (steps, steps), 1) <= lax.broadcasted_iota(jnp.int32, (steps, steps), 0)
    slot_id = lax.broadcasted_iota(jnp.int32, (steps, shard), 1)

    def rs_copy(b, d):
        to = lax.rem(chip + d, chips)
        return remote(yp.at[b, :, pl.ds(pl.multiple_of(to * block, block), block)], rs.at[b, d - 1], rs_send.at[b, d - 1], rs_recv.at[b, d - 1], to * CORES + core)

    def o_copy(b):
        return remote(o_own.at[b], o_peer.at[b], o_send.at[b], o_recv.at[b], partner)

    @pl.loop(0, rows)
    def _(b):
        own_copy(0, b).wait()
        for n in range(len(hops)):
            cache_copy(0, b, n).wait_recv()
        length = plen_ref[b]

        @pl.loop(0, heads)
        def _(h):
            q = qs[b, h]
            peak = jnp.full((steps, shard), -jnp.inf, F32)
            for s in range(parts):
                scores = dot_t(q, kf[b, h, s * shard:(s + 1) * shard, :])
                scores = jnp.where(slot_id < length - s * shard, scores, -jnp.inf)
                sc[:, s * shard:(s + 1) * shard] = scores
                peak = jnp.maximum(peak, scores)
            fresh = jnp.where(causal, dot_t(q, kn[b, h]), -jnp.inf)
            row_peak = jnp.maximum(jnp.max(peak, axis=-1, keepdims=True), jnp.max(fresh, axis=-1, keepdims=True))
            total = jnp.zeros((steps, shard), F32)
            for s in range(parts):
                e = jnp.exp(sc[:, s * shard:(s + 1) * shard] - row_peak)
                sc[:, s * shard:(s + 1) * shard] = e
                total = total + e
            fresh = jnp.exp(fresh - row_peak)
            inv = 1.0 / (jnp.sum(total, axis=-1, keepdims=True) + jnp.sum(fresh, axis=-1, keepdims=True))
            for s in range(parts):
                pb[h, :, s * shard:(s + 1) * shard] = (sc[:, s * shard:(s + 1) * shard] * inv).astype(BF16)
            pn[h] = (fresh * inv).astype(BF16)

        own_copy(1, b).wait()
        for n in range(len(hops)):
            cache_copy(1, b, n).wait_recv()

        for h in range(heads):
            out = dot(pn[h], vn[b, h]) + dot(pb[h], vf[b, h, :seq_len, :])
            o_own[b, :, h * head_dim:(h + 1) * head_dim] = out.astype(BF16)
        o_copy(b).start()
        o_copy(b).wait_recv()
        for j in range(chips):
            cols = slice(j * block, (j + 1) * block)
            part = dot(o_own[b], wo_own[:, cols]) + dot(o_peer[b], wo_peer[:, cols])
            yp[b, :, cols] = part.astype(BF16)
        for d in range(1, chips):
            rs_copy(b, d).start()

    def columns(which_core, which_chip):
        return pl.ds(pl.multiple_of(which_core * half + which_chip * block, block), block)

    def ag_copy(b, d):
        to = lax.rem(chip + d, chips)
        mine = yf.at[b, :, columns(core, chip)]
        return remote(mine, mine, ag_send.at[b, d - 1], ag_recv.at[b, d - 1], to * CORES + core)

    def d_copy(b):
        mine = yf.at[b, :, half_cols(core)]
        return remote(mine, mine, d_send.at[b], d_recv.at[b], partner)

    for b in range(rows):
        for d in range(1, chips):
            rs_copy(b, d).wait_recv()
        attn = yp[b, :, pl.ds(pl.multiple_of(chip * block, block), block)].astype(F32)
        for d in range(1, chips):
            attn = attn + rs[b, d - 1].astype(F32)
        yf[b, :, columns(core, chip)] = (xs[b, :, columns(core, chip)].astype(F32) + attn).astype(BF16)
        for d in range(1, chips):
            ag_copy(b, d).start()
    for b in range(rows):
        for d in range(1, chips):
            ag_copy(b, d).wait_recv()
        d_copy(b).start()
    for b in range(rows):
        d_copy(b).wait()
        o_copy(b).wait_send()
        for d in range(1, chips):
            rs_copy(b, d).wait_send()
            ag_copy(b, d).wait_send()
        for kind in range(2):
            for n in range(len(hops)):
                cache_copy(kind, b, n).wait_send()


def write_kernel(plen_ref, kf, vf, kn, vn, yf, k_out, v_out, y_out, win, ys, big_sem, win_sem, y_sem):
    rows, heads, steps, head_dim = kn.shape
    out_len = kf.shape[2]
    span = win.shape[3]
    last = out_len - span

    def start_of(b):
        p = plen_ref[b]
        return pl.multiple_of(jnp.minimum(p - lax.rem(p, WINDOW_ALIGN), last), WINDOW_ALIGN)

    def big(kind, b):
        src, dst = ((kf, k_out), (vf, v_out))[kind]
        return pltpu.make_async_copy(src.at[b], dst.at[b], big_sem.at[kind, b])

    def small(kind, b):
        return pltpu.make_async_copy(win.at[kind, b], (k_out, v_out)[kind].at[b, :, pl.ds(start_of(b), span), :], win_sem.at[kind, b])

    for b in range(rows):
        for kind in range(2):
            big(kind, b).start()
    for b in range(rows):
        ys[:, b, :] = yf[b]
    y_copy = pltpu.make_async_copy(ys, y_out, y_sem)
    y_copy.start()
    row_id = lax.broadcasted_iota(jnp.int32, (span, steps), 0)
    col_id = lax.broadcasted_iota(jnp.int32, (span, steps), 1)
    pos = lax.broadcasted_iota(jnp.int32, (span, head_dim), 0)
    for b in range(rows):
        start = start_of(b)
        offset = plen_ref[b] - start
        select = (row_id == col_id + offset).astype(BF16)
        fresh = (pos >= offset) & (pos < offset + steps)
        for kind in range(2):
            old, new = ((kf, kn), (vf, vn))[kind]
            for h in range(heads):
                moved = dot(select, new[b, h])
                kept = old[b, h, pl.ds(start, span), :].astype(F32)
                win[kind, b, h] = jnp.where(fresh, moved, kept).astype(BF16)
    for b in range(rows):
        for kind in range(2):
            big(kind, b).wait()
            small(kind, b).start()
    y_copy.wait()
    for b in range(rows):
        for kind in range(2):
            small(kind, b).wait()


def solution(mesh):
    parts = mesh.shape["tp"]
    chips = parts // CORES

    def local_block(k_cache, v_cache, prompt_len, x_steps, w_norm, w_q, w_k, w_v, w_o):
        rows, _, shard, head_dim = k_cache.shape
        steps, _, model = x_steps.shape
        width = w_q.shape[1]
        heads = width // head_dim
        seq_len = shard * parts
        out_len = seq_len + steps
        half = model // CORES
        block = half // chips
        half_dim = head_dim // 2
        inv_freq = ROPE_BASE ** (-2.0 * jnp.arange(half_dim, dtype=F32) / head_dim)
        positions = prompt_len[:, None] + jnp.arange(steps)[None, :]
        angles = positions.astype(F32)[..., None] * inv_freq
        cos, sin = jnp.cos(angles), jnp.sin(angles)
        cos_full = jnp.concatenate([cos, cos], axis=-1)
        sin_full = jnp.concatenate([-sin, sin], axis=-1)
        dma = pltpu.SemaphoreType.DMA
        peers = parts - 1
        kf, vf, kn, vn, yf = pl.pallas_call(
            functools.partial(exchange_kernel, chips, steps),
            out_shape=(
                pltpu.VMEM((rows, heads, out_len, head_dim), BF16),
                pltpu.VMEM((rows, heads, out_len, head_dim), BF16),
                pltpu.VMEM((rows, heads, steps, head_dim), BF16),
                pltpu.VMEM((rows, heads, steps, head_dim), BF16),
                pltpu.VMEM((rows, steps, model), BF16),
            ),
            in_specs=[SMEM] + [ANY] * 10,
            out_specs=(VMEM,) * 5,
            scratch_shapes=[
                pltpu.VMEM((WINDOW_ALIGN, rows, model), BF16),
                pltpu.VMEM((rows, steps, model), BF16),
                pltpu.VMEM((1, model), BF16),
                pltpu.VMEM((rows, steps, head_dim), F32),
                pltpu.VMEM((rows, steps, head_dim), F32),
                pltpu.VMEM((rows * steps, model), BF16),
                pltpu.VMEM((2, model, 2 * head_dim), BF16),
                pltpu.VMEM((width, half), BF16),
                pltpu.VMEM((width, half), BF16),
                pltpu.VMEM((rows, heads, steps, head_dim), BF16),
                pltpu.VMEM((steps, seq_len), F32),
                pltpu.VMEM((heads, steps, seq_len), BF16),
                pltpu.VMEM((heads, steps, steps), BF16),
                pltpu.VMEM((rows, steps, width), BF16),
                pltpu.VMEM((rows, steps, width), BF16),
                pltpu.VMEM((rows, steps, half), BF16),
                pltpu.VMEM((rows, chips - 1, steps, block), BF16),
                dma((2, rows, peers)),
                dma((2, rows, peers)),
                dma((2, rows)),
                dma((6,)),
                dma((5,)),
                dma((2,)),
                dma((rows,)),
                dma((rows,)),
                dma((rows, chips - 1)),
                dma((rows, chips - 1)),
                dma((rows, chips - 1)),
                dma((rows, chips - 1)),
                dma((rows,)),
                dma((rows,)),
            ],
            compiler_params=pltpu.CompilerParams(collective_id=0, has_side_effects=True, vmem_limit_bytes=28 << 20),
        )(prompt_len, k_cache, v_cache, x_steps, w_norm.reshape(1, model), w_q, w_k, w_v, w_o, cos_full, sin_full)
        span = steps + WINDOW_ALIGN
        k_out, v_out, y = pl.pallas_call(
            write_kernel,
            out_shape=(
                jax.ShapeDtypeStruct((rows, heads, out_len, head_dim), BF16),
                jax.ShapeDtypeStruct((rows, heads, out_len, head_dim), BF16),
                jax.ShapeDtypeStruct((steps, rows, model), BF16),
            ),
            in_specs=[SMEM] + [VMEM] * 5,
            out_specs=(ANY,) * 3,
            scratch_shapes=[
                pltpu.VMEM((2, rows, heads, span, head_dim), BF16),
                pltpu.VMEM((steps, rows, model), BF16),
                dma((2, rows)),
                dma((2, rows)),
                dma,
            ],
            compiler_params=pltpu.CompilerParams(vmem_limit_bytes=16 << 20),
        )(prompt_len, kf, vf, kn, vn, yf)
        return y, k_out, v_out

    cache_spec = P("dp", None, "tp", None)
    col_spec = P(None, "tp")
    out_cache_spec = P("dp", "tp", None, None)
    return jax.shard_map(local_block, mesh=mesh, in_specs=(cache_spec, cache_spec, P("dp"), P(None, "dp", None), P(None), col_spec, col_spec, col_spec, P("tp", None)), out_specs=(P(None, "dp", None), out_cache_spec, out_cache_spec), check_vma=False)
```

time: 542 us -> 435 us (0.80)
  Pallas kernels: 0 us -> 406 us
  waiting for transfers between devices: 303 us -> 0 us
  local copies, waits for them, and re-layouts: 108 us -> 25.5 us
  other arithmetic: 63.2 us -> 2.11 us
  matrix products: 38.2 us -> 0 us
  starting transfers between devices: 13.4 us -> 0 us
  between operations: 14.2 us -> 0.82 us
    pallas_call x0 -> x2, Pallas kernels: none -> 406 us  [the longest x1 394 us: local_block(): pl.pallas_call(functools.partial(exchange_kernel, chips, steps), out_shap...]
    all_to_all x2 -> x0, waiting for transfers between devices: 303 us -> none  [the longest x1 169 us: local_block(): k_heads = lax.all_to_all(k_cache, 'tp', 1, 2, tiled=True)]
    scatter x17 -> x0, other arithmetic: 47.2 us -> none
    dot_general x7 -> x0, matrix products: 38.2 us -> none  [the longest x1 15.8 us: decode_heads(): jnp.einsum('bhsd,hdm->sbm', heads_out.astype(jnp.bfloat16), w_o.reshape(n...]
    scatter x24 -> x0, local copies, waits for them, and re-layouts: 27.3 us -> none
    concatenate x2 -> x0, local copies, waits for them, and re-layouts: 25.6 us -> none  [the longest x1 19 us: decode_heads(): jnp.concatenate([k_heads, zero_tail], axis=2)]
    all_to_all x2 -> x0, local copies, waits for them, and re-layouts: 22.5 us -> none  [the longest x1 14.2 us: local_block(): k_heads = lax.all_to_all(k_cache, 'tp', 1, 2, tiled=True)]
    all_to_all x2 -> x0, starting transfers between devices: 13.4 us -> none  [the longest x1 7.04 us: local_block(): v_heads = lax.all_to_all(v_cache, 'tp', 1, 2, tiled=True)]
  transfers between devices with their start and end apart: 3 -> 0, of which waited for: 2 -> 0; matrix products, arithmetic and copies ran while one was open for 25% -> 0% of each run, Pallas kernels for 0% -> 0%
where the time goes in v1:
time: 435 us; the launch traced here: 434 us
  Pallas kernels  406 us (93%)
  local copies, waits for them, and re-layouts  25.5 us (6%)
    pallas_call x1, Pallas kernels, local_block(): pl.pallas_call(functools.partial(exchange_kernel, chips, steps), out_shap...  394 us
    unnamed x10, local copies, waits for them, and re-layouts  24.2 us
    pallas_call x1, Pallas kernels, local_block(): pl.pallas_call(write_kernel, out_shape=(jax.ShapeDtypeStruct((rows, heads...  12.5 us

profile of v1, /device:TPU:113, one launch (start us, length us, event | category | flops | bytes accessed | tf_op | source)
XLA Modules:
  0.0 434.4 jit_solution(12738143146927788787)
XLA Ops:
  0.6 0.7 add_convert_fusion
  1.4 1.3 reshape.36.gain_ref
  2.7 0.5 fusion
  3.2 0.8 pad_maximum_fusion
  4.1 0.0 copy-start.4
  4.1 393.5 %shard_map.112 = (bf16[4,4,4160,128]{3,2,1,0:T(8,128)(2,1)S(1)}, bf16[4,4,4160,128]{3,2,1,0:T(8,128)(2,1)S(1)}, bf16[4,4,64,128]{3,2,1,0:T(8,128)(2,1)S(1)}, bf1...) custom-call(s32[4]{0:T(128)} %plen_ref.3, bf16[4,32,512,128]{3,2,1,0:T(8,128)(2,1)} %k_ref.1, ...), custom_call_target="tpu_custom_call" | custom-call | tf_op jit(solution)/shard_map/pallas_call | solution.py:301
  397.6 0.0 copy-start
  397.6 6.2 %copy-done = bf16[4,4,4160,128]{3,2,1,0:T(8,128)(2,1)} copy-done((bf16[4,4,4160,128]{3,2,1,0:T(8,128)(2,1)}, bf16[4,4,4160,128]{3,2,1,0:T(8,128)(2,1)S(1)}, u32[]{:S(2)}) %copy-start) | copy-done | bytes 17039384
  403.8 0.0 copy-start.2
  403.8 6.2 %copy-done.2 = bf16[4,4,4160,128]{3,2,1,0:T(8,128)(2,1)} copy-done((bf16[4,4,4160,128]{3,2,1,0:T(8,128)(2,1)}, bf16[4,4,4160,128]{3,2,1,0:T(8,128)(2,1)S(1)}, u32[]{:S(2)}) %copy-start.2) | copy-done | bytes 17039384
  410.1 0.0 copy-done.4
  410.1 0.0 copy-start.1
  410.1 5.8 %copy-done.1 = bf16[4,4,4160,128]{3,2,1,0:T(8,128)(2,1)S(1)} copy-done((bf16[4,4,4160,128]{3,2,1,0:T(8,128)(2,1)S(1)}, bf16[4,4,4160,128]{3,2,1,0:T(8,128)(2,1)}, u32[]{:S(2)}) %copy-start.1) | copy-done | bytes 17039384
  415.9 0.0 copy-start.3
  415.9 5.8 %copy-done.3 = bf16[4,4,4160,128]{3,2,1,0:T(8,128)(2,1)S(1)} copy-done((bf16[4,4,4160,128]{3,2,1,0:T(8,128)(2,1)S(1)}, bf16[4,4,4160,128]{3,2,1,0:T(8,128)(2,1)}, u32[]{:S(2)}) %copy-start.3) | copy-done | bytes 17039384
  421.8 12.5 %shard_map.113 = (bf16[4,4,4160,128]{3,2,1,0:T(8,128)(2,1)}, bf16[4,4,4160,128]{3,2,1,0:T(8,128)(2,1)}, bf16[64,4,4096]{2,1,0:T(4,128)(2,1)}) custom-call(s32[4]{0:T(128)S(1)} %copy-done.4, bf16[4,4,4160,128]{3,2,1,0:T(8,128)(2,1)S(1)} %copy-done.1, bf16[4,4,4160,128]{3,2,1,0:T(8,128)(2,1)S(1)} %copy-done.3, ...), custom_call_target="tpu_custom_call" | custom-call | tf_op jit(solution)/shard_map/pallas_call | solution.py:348
  (1 shorter events, 0.0 us)
Async XLA Ops:
  4.1 406.0 %copy-start.4 = (s32[4]{0:T(128)S(1)}, s32[4]{0:T(128)}, u32[]{:S(2)}) copy-start(s32[4]{0:T(128)} %plen_ref.3) | copy-start | bytes 52
  397.6 6.2 %copy-start = (bf16[4,4,4160,128]{3,2,1,0:T(8,128)(2,1)}, bf16[4,4,4160,128]{3,2,1,0:T(8,128)(2,1)S(1)}, u32[]{:S(2)}) copy-start(bf16[4,4,4160,128]{3,2,1,0:T(8,128)(2,1)S(1)} %get-tuple-element.11.kf) | copy-start | bytes 51118084
  403.8 6.2 %copy-start.2 = (bf16[4,4,4160,128]{3,2,1,0:T(8,128)(2,1)}, bf16[4,4,4160,128]{3,2,1,0:T(8,128)(2,1)S(1)}, u32[]{:S(2)}) copy-start(bf16[4,4,4160,128]{3,2,1,0:T(8,128)(2,1)S(1)} %get-tuple-element.12.vf) | copy-start | bytes 51118084
  410.1 5.8 %copy-start.1 = (bf16[4,4,4160,128]{3,2,1,0:T(8,128)(2,1)S(1)}, bf16[4,4,4160,128]{3,2,1,0:T(8,128)(2,1)}, u32[]{:S(2)}) copy-start(bf16[4,4,4160,128]{3,2,1,0:T(8,128)(2,1)} %copy-done) | copy-start | bytes 51118084
  415.9 5.8 %copy-start.3 = (bf16[4,4,4160,128]{3,2,1,0:T(8,128)(2,1)S(1)}, bf16[4,4,4160,128]{3,2,1,0:T(8,128)(2,1)}, u32[]{:S(2)}) copy-start(bf16[4,4,4160,128]{3,2,1,0:T(8,128)(2,1)} %copy-done.2) | copy-start | bytes 51118084

commit v2 on v1

--- a/solution.py
+++ b/solution.py
@@ -2,6 +2,7 @@
 
 import jax
 import jax.numpy as jnp
+import numpy as np
 from jax import lax
 from jax.experimental import pallas as pl
 from jax.experimental.pallas import tpu as pltpu
@@ -11,6 +12,8 @@
 NORM_EPS = 1e-6
 CORES = 2
 WINDOW_ALIGN = 16
+STAGE_STEPS = 8
+VMEM_LIMIT = 12480 << 10
 MESH = pl.DeviceIdType.MESH
 F32 = jnp.float32
 BF16 = jnp.bfloat16
@@ -30,7 +33,7 @@
 def exchange_kernel(
     chips, steps, plen_ref, k_ref, v_ref, x_ref, gain_ref, wq_ref, wk_ref, wv_ref, wo_ref, cos_ref, sin_ref,
     kf, vf, kn, vn, yf,
-    stage, xs, gs, cs, sn, hs, wb, wo_own, wo_peer, qs, sc, pb, pn, o_own, o_peer, yp, rs,
+    stage, gs, hp, wb, sc, pn, xs, wo_own, wo_peer, qs, o_peer, rs,
     kv_send, kv_recv, kv_own, w_sem, in_sem, wo_sems, o_send, o_recv, rs_send, rs_recv, ag_send, ag_recv, d_send, d_recv,
 ):
     rows, heads, _, head_dim = kn.shape
@@ -82,70 +85,97 @@
             for n in range(len(hops)):
                 cache_copy(kind, b, n).start()
 
+    for b in range(rows):
+        for kind in range(2):
+            own_copy(kind, b).start()
+    wo_load = pltpu.make_async_copy(wo_ref.at[:, half_cols(core)], wo_own, in_sem.at[3])
+    wo_load.start()
+    zero_tail = jnp.zeros((rows, heads, steps, head_dim), BF16)
+    kf[:, :, seq_len:, :] = zero_tail
+    vf[:, :, seq_len:, :] = zero_tail
+
+    def columns(which_core, which_chip):
+        return pl.ds(pl.multiple_of(which_core * half + which_chip * block, block), block)
+
     loads = [
         pltpu.make_async_copy(gain_ref, gs, in_sem.at[0]),
-        pltpu.make_async_copy(cos_ref, cs, in_sem.at[1]),
-        pltpu.make_async_copy(sin_ref, sn, in_sem.at[2]),
-        pltpu.make_async_copy(wo_ref.at[:, half_cols(core)], wo_own, in_sem.at[3]),
+        pltpu.make_async_copy(cos_ref, sc.at[:, :rows * head_dim], in_sem.at[1]),
+        pltpu.make_async_copy(sin_ref, sc.at[:, rows * head_dim:2 * rows * head_dim], in_sem.at[2]),
     ]
     for c in loads:
         c.start()
-    pair = wb.shape[2]
-    groups = width // pair
+    groups = width // head_dim
     w_loads = [
-        pltpu.make_async_copy((wq_ref, wk_ref, wv_ref)[i // groups].at[:, i % groups * pair:(i % groups + 1) * pair], wb.at[i % 2], w_sem.at[i])
+        pltpu.make_async_copy((wq_ref, wk_ref, wv_ref)[i // groups].at[:, i % groups * head_dim:(i % groups + 1) * head_dim], wb.at[i % 2], w_sem.at[i])
         for i in range(3 * groups)
     ]
     w_loads[0].start()
     w_loads[1].start()
-    for b in range(rows):
-        for kind in range(2):
-            own_copy(kind, b).start()
-    zero_tail = jnp.zeros((rows, heads, steps, head_dim), BF16)
-    kf[:, :, seq_len:, :] = zero_tail
-    vf[:, :, seq_len:, :] = zero_tail
     for c in loads:
         c.wait()
 
-    gain = 1.0 + gs[...].astype(F32)
     part_steps = stage.shape[0]
     for t in range(0, steps, part_steps):
         x_load = pltpu.make_async_copy(x_ref.at[t:t + part_steps], stage, in_sem.at[4])
         x_load.start()
         x_load.wait()
+
         for b in range(rows):
-            x = stage[:, b, :]
-            xs[b, t:t + part_steps, :] = x
-            residual = x.astype(F32)
-            inv_rms = lax.rsqrt(jnp.mean(residual * residual, axis=-1, keepdims=True) + NORM_EPS)
-            hs[b * steps + t:b * steps + t + part_steps, :] = (residual * inv_rms * gain).astype(BF16)
+            xs[b, t:t + part_steps, :] = stage[:, b, columns(core, chip)]
+            squares = jnp.zeros((part_steps, block), F32)
+            for c in range(0, model, block):
+                residual = stage[:, b, c:c + block].astype(F32)
+                squares = squares + residual * residual
+            inv_rms = lax.rsqrt(jnp.sum(squares, axis=-1, keepdims=True) * (1.0 / model) + NORM_EPS)
+            for c in range(0, model, block):
+                residual = stage[:, b, c:c + block].astype(F32)
+                gain = 1.0 + gs[c:c + block].astype(F32).reshape(1, block)
+                hp[b * steps + t:b * steps + t + part_steps, c:c + block] = (residual * inv_rms * gain).astype(BF16)
+
+    def lane_tile(n):
+        return pl.ds(pl.multiple_of(n * head_dim, head_dim), head_dim)
 
     for i, load in enumerate(w_loads):
         load.wait()
         matrix, j = i // groups, i % groups
-        flat = dot(hs[...], wb[i % 2]).astype(BF16)
+
+        @pl.loop(0, rows)
+        def _(b, i=i, matrix=matrix, j=j):
+            u = dot(hp[pl.ds(pl.multiple_of(b * steps, steps), steps), :model], wb[i % 2]).astype(BF16)
+            if matrix < 2:
+                u = u.astype(F32)
+                u = u * sc[:, lane_tile(b)] + pltpu.roll(u, head_dim // 2, 1) * sc[:, lane_tile(rows + b)]
+                if matrix == 0:
+                    u = u * head_dim ** -0.5
+            (qs, kn, vn)[matrix][b, j] = u.astype(BF16)
+
         if i + 2 < len(w_loads):
             w_loads[i + 2].start()
-        for sub in range(pair // head_dim):
-            for b in range(rows):
-                u = flat[b * steps:(b + 1) * steps, sub * head_dim:(sub + 1) * head_dim]
-                if matrix < 2:
-                    u = u.astype(F32)
-                    u = u * cs[b] + pltpu.roll(u, head_dim // 2, 1) * sn[b]
-                    if matrix == 0:
-                        u = u * head_dim ** -0.5
-                (qs, kn, vn)[matrix][b, j * (pair // head_dim) + sub] = u.astype(BF16)
-
+
+    wo_load.wait()
     wo_send.wait()
     causal = lax.broadcasted_iota(jnp.int32, (steps, steps), 1) <= lax.broadcasted_iota(jnp.int32, (steps, steps), 0)
     slot_id = lax.broadcasted_iota(jnp.int32, (steps, shard), 1)
 
+    lanes = wb.shape[2]
+    tiles = block // lanes
+
+    def head_rows(h):
+        return pl.ds(pl.multiple_of(h * steps, steps), steps)
+
+    def partial_rows(b, which_chip, tile=0, count=1):
+        first = ((b * chips + which_chip) * tiles + tile) * steps
+        return pl.ds(pl.multiple_of(first, steps), count * steps)
+
     def rs_copy(b, d):
         to = lax.rem(chip + d, chips)
-        return remote(yp.at[b, :, pl.ds(pl.multiple_of(to * block, block), block)], rs.at[b, d - 1], rs_send.at[b, d - 1], rs_recv.at[b, d - 1], to * CORES + core)
+        return remote(wb.at[0, partial_rows(b, to, 0, tiles)], rs.at[b, d - 1], rs_send.at[b, d - 1], rs_recv.at[b, d - 1], to * CORES + core)
+
+    def head_tile(b, h, count=1):
+        return pl.ds(pl.multiple_of((b * heads + h) * steps, steps), count * steps)
 
     def o_copy(b):
-        return remote(o_own.at[b], o_peer.at[b], o_send.at[b], o_recv.at[b], partner)
+        return remote(wb.at[1, head_tile(b, 0, heads)], o_peer.at[b], o_send.at[b], o_recv.at[b], partner)
 
     @pl.loop(0, rows)
     def _(b):
@@ -157,43 +187,61 @@
         @pl.loop(0, heads)
         def _(h):
             q = qs[b, h]
-            peak = jnp.full((steps, shard), -jnp.inf, F32)
-            for s in range(parts):
-                scores = dot_t(q, kf[b, h, s * shard:(s + 1) * shard, :])
+
+            def score(s, peak):
+                cols = pl.ds(pl.multiple_of(s * shard, shard), shard)
+                scores = dot_t(q, kf[b, h, cols, :])
                 scores = jnp.where(slot_id < length - s * shard, scores, -jnp.inf)
-                sc[:, s * shard:(s + 1) * shard] = scores
-                peak = jnp.maximum(peak, scores)
+                sc[:, cols] = scores
+                return jnp.maximum(peak, scores)
+
+            peak = lax.fori_loop(0, parts, score, jnp.full((steps, shard), -jnp.inf, F32))
             fresh = jnp.where(causal, dot_t(q, kn[b, h]), -jnp.inf)
             row_peak = jnp.maximum(jnp.max(peak, axis=-1, keepdims=True), jnp.max(fresh, axis=-1, keepdims=True))
-            total = jnp.zeros((steps, shard), F32)
-            for s in range(parts):
-                e = jnp.exp(sc[:, s * shard:(s + 1) * shard] - row_peak)
-                sc[:, s * shard:(s + 1) * shard] = e
-                total = total + e
+
+            def exponent(s, total):
+                cols = pl.ds(pl.multiple_of(s * shard, shard), shard)
+                e = jnp.exp(sc[:, cols] - row_peak)
+                sc[:, cols] = e
+                return total + e
+
+            total = lax.fori_loop(0, parts, exponent, jnp.zeros((steps, shard), F32))
             fresh = jnp.exp(fresh - row_peak)
             inv = 1.0 / (jnp.sum(total, axis=-1, keepdims=True) + jnp.sum(fresh, axis=-1, keepdims=True))
-            for s in range(parts):
-                pb[h, :, s * shard:(s + 1) * shard] = (sc[:, s * shard:(s + 1) * shard] * inv).astype(BF16)
+
+            @pl.loop(0, parts)
+            def _(s):
+                cols = pl.ds(pl.multiple_of(s * shard, shard), shard)
+                hp[head_rows(h), cols] = (sc[:, cols] * inv).astype(BF16)
+
             pn[h] = (fresh * inv).astype(BF16)
 
         own_copy(1, b).wait()
         for n in range(len(hops)):
             cache_copy(1, b, n).wait_recv()
 
-        for h in range(heads):
-            out = dot(pn[h], vn[b, h]) + dot(pb[h], vf[b, h, :seq_len, :])
-            o_own[b, :, h * head_dim:(h + 1) * head_dim] = out.astype(BF16)
+        @pl.loop(0, heads)
+        def _(h):
+            out = dot(pn[h], vn[b, h])
+            for s in range(parts):
+                cols = slice(s * shard, (s + 1) * shard)
+                out = out + dot(hp[head_rows(h), cols], vf[b, h, cols, :])
+            wb[1, head_tile(b, h)] = out.astype(BF16)
+
         o_copy(b).start()
         o_copy(b).wait_recv()
-        for j in range(chips):
-            cols = slice(j * block, (j + 1) * block)
-            part = dot(o_own[b], wo_own[:, cols]) + dot(o_peer[b], wo_peer[:, cols])
-            yp[b, :, cols] = part.astype(BF16)
+
+        @pl.loop(0, chips)
+        def _(j):
+            cols = pl.ds(pl.multiple_of(j * block, block), block)
+            own = jnp.concatenate([wb[1, head_tile(b, h)] for h in range(heads)], axis=1)
+            other = jnp.concatenate([o_peer[b, h * steps:(h + 1) * steps] for h in range(heads)], axis=1)
+            part = (dot(own, wo_own[:, cols]) + dot(other, wo_peer[:, cols])).astype(BF16)
+            for tile in range(tiles):
+                wb[0, partial_rows(b, j, tile)] = part[:, tile * lanes:(tile + 1) * lanes]
+
         for d in range(1, chips):
             rs_copy(b, d).start()
-
-    def columns(which_core, which_chip):
-        return pl.ds(pl.multiple_of(which_core * half + which_chip * block, block), block)
 
     def ag_copy(b, d):
         to = lax.rem(chip + d, chips)
@@ -207,10 +255,13 @@
     for b in range(rows):
         for d in range(1, chips):
             rs_copy(b, d).wait_recv()
-        attn = yp[b, :, pl.ds(pl.multiple_of(chip * block, block), block)].astype(F32)
-        for d in range(1, chips):
-            attn = attn + rs[b, d - 1].astype(F32)
-        yf[b, :, columns(core, chip)] = (xs[b, :, columns(core, chip)].astype(F32) + attn).astype(BF16)
+        for tile in range(tiles):
+            cols = slice(tile * lanes, (tile + 1) * lanes)
+            attn = wb[0, partial_rows(b, chip, tile)].astype(F32)
+            for d in range(1, chips):
+                attn = attn + rs[b, d - 1, tile * steps:(tile + 1) * steps].astype(F32)
+            out_cols = pl.ds(pl.multiple_of(core * half + chip * block + tile * lanes, lanes), lanes)
+            yf[b, :, out_cols] = (xs[b, :, cols].astype(F32) + attn).astype(BF16)
         for d in range(1, chips):
             ag_copy(b, d).start()
     for b in range(rows):
@@ -289,13 +340,13 @@
         out_len = seq_len + steps
         half = model // CORES
         block = half // chips
+        tiles = block // head_dim
         half_dim = head_dim // 2
-        inv_freq = ROPE_BASE ** (-2.0 * jnp.arange(half_dim, dtype=F32) / head_dim)
-        positions = prompt_len[:, None] + jnp.arange(steps)[None, :]
-        angles = positions.astype(F32)[..., None] * inv_freq
-        cos, sin = jnp.cos(angles), jnp.sin(angles)
-        cos_full = jnp.concatenate([cos, cos], axis=-1)
-        sin_full = jnp.concatenate([-sin, sin], axis=-1)
+        inv_freq = (ROPE_BASE ** (-2.0 * np.arange(half_dim) / head_dim)).astype(np.float32)
+        sign = np.where(np.arange(head_dim) < half_dim, -1.0, 1.0).astype(np.float32)
+        starts = jnp.broadcast_to(prompt_len[:, None], (rows, head_dim)).reshape(1, rows * head_dim)
+        angles = (jnp.arange(steps)[:, None] + starts).astype(F32) * np.tile(inv_freq, 2 * rows)
+        cos, sin = jnp.cos(angles), jnp.sin(angles) * np.tile(sign, rows)
         dma = pltpu.SemaphoreType.DMA
         peers = parts - 1
         kf, vf, kn, vn, yf = pl.pallas_call(
@@ -310,27 +361,22 @@
             in_specs=[SMEM] + [ANY] * 10,
             out_specs=(VMEM,) * 5,
             scratch_shapes=[
-                pltpu.VMEM((WINDOW_ALIGN, rows, model), BF16),
-                pltpu.VMEM((rows, steps, model), BF16),
-                pltpu.VMEM((1, model), BF16),
-                pltpu.VMEM((rows, steps, head_dim), F32),
-                pltpu.VMEM((rows, steps, head_dim), F32),
-                pltpu.VMEM((rows * steps, model), BF16),
-                pltpu.VMEM((2, model, 2 * head_dim), BF16),
+                pltpu.VMEM((STAGE_STEPS, rows, model), BF16),
+                pltpu.VMEM((model,), BF16),
+                pltpu.VMEM((max(rows, heads) * steps, max(model, seq_len)), BF16),
+                pltpu.VMEM((2, model, head_dim), BF16),
+                pltpu.VMEM((steps, seq_len), F32),
+                pltpu.VMEM((heads, steps, steps), BF16),
+                pltpu.VMEM((rows, steps, block), BF16),
                 pltpu.VMEM((width, half), BF16),
                 pltpu.VMEM((width, half), BF16),
                 pltpu.VMEM((rows, heads, steps, head_dim), BF16),
-                pltpu.VMEM((steps, seq_len), F32),
-                pltpu.VMEM((heads, steps, seq_len), BF16),
-                pltpu.VMEM((heads, steps, steps), BF16),
-                pltpu.VMEM((rows, steps, width), BF16),
-                pltpu.VMEM((rows, steps, width), BF16),
-                pltpu.VMEM((rows, steps, half), BF16),
-                pltpu.VMEM((rows, chips - 1, steps, block), BF16),
+                pltpu.VMEM((rows, heads * steps, head_dim), BF16),
+                pltpu.VMEM((rows, chips - 1, tiles * steps, head_dim), BF16),
                 dma((2, rows, peers)),
                 dma((2, rows, peers)),
                 dma((2, rows)),
-                dma((6,)),
+                dma((3 * width // head_dim,)),
                 dma((5,)),
                 dma((2,)),
                 dma((rows,)),
@@ -342,8 +388,8 @@
                 dma((rows,)),
                 dma((rows,)),
             ],
-            compiler_params=pltpu.CompilerParams(collective_id=0, has_side_effects=True, vmem_limit_bytes=28 << 20),
-        )(prompt_len, k_cache, v_cache, x_steps, w_norm.reshape(1, model), w_q, w_k, w_v, w_o, cos_full, sin_full)
+            compiler_params=pltpu.CompilerParams(collective_id=0, has_side_effects=True, vmem_limit_bytes=VMEM_LIMIT),
+        )(prompt_len, *(pltpu.with_memory_space_constraint(a, pltpu.HBM) for a in (k_cache, v_cache, x_steps, w_norm, w_q, w_k, w_v, w_o)), cos, sin)
         span = steps + WINDOW_ALIGN
         k_out, v_out, y = pl.pallas_call(
             write_kernel,
@@ -361,7 +407,7 @@
                 dma((2, rows)),
                 dma,
             ],
-            compiler_params=pltpu.CompilerParams(vmem_limit_bytes=16 << 20),
+            compiler_params=pltpu.CompilerParams(vmem_limit_bytes=6 << 20),
         )(prompt_len, kf, vf, kn, vn, yf)
         return y, k_out, v_out
 

time: 435 us -> 409 us (0.940)
  local copies, waits for them, and re-layouts: 25.5 us -> 1.38 us
    unnamed x10 -> x2, local copies, waits for them, and re-layouts: 24.2 us -> 0.65 us
where the time goes in v2:
time: 409 us
  Pallas kernels  406 us (99%)
    pallas_call x1, Pallas kernels, local_block(): pl.pallas_call(functools.partial(exchange_kernel, chips, steps), out_shap...  393 us
    pallas_call x1, Pallas kernels, local_block(): pl.pallas_call(write_kernel, out_shape=(jax.ShapeDtypeStruct((rows, heads...  12.5 us

profile of v2, /device:TPU:113, one launch (start us, length us, event | category | flops | bytes accessed | tf_op | source)
XLA Modules:
  0.0 409.0 jit_solution(3196708139202330029)
XLA Ops:
  0.6 0.7 broadcast_bitcast_fusion
  1.4 1.2 sine_multiply_fusion
  2.5 0.0 copy-start
  2.6 0.6 copy-done
  3.2 393.3 %shard_map.130 = (bf16[4,4,4160,128]{3,2,1,0:T(8,128)(2,1)S(1)}, bf16[4,4,4160,128]{3,2,1,0:T(8,128)(2,1)S(1)}, bf16[4,4,64,128]{3,2,1,0:T(8,128)(2,1)S(1)}, bf1...) custom-call(s32[4]{0:T(128)S(1)} %copy-done, bf16[4,32,512,128]{3,2,1,0:T(8,128)(2,1)} %k_ref.1, ...), custom_call_target="tpu_custom_call" | custom-call | tf_op jit(solution)/shard_map/pallas_call | solution.py:352
  396.5 12.5 %shard_map.131 = (bf16[4,4,4160,128]{3,2,1,0:T(8,128)(2,1)}, bf16[4,4,4160,128]{3,2,1,0:T(8,128)(2,1)}, bf16[64,4,4096]{2,1,0:T(4,128)(2,1)}) custom-call(s32[4]{0:T(128)S(1)} %copy-done, bf16[4,4,4160,128]{3,2,1,0:T(8,128)(2,1)S(1)} %get-tuple-element.11.kf, bf16[4,4,4160,128]{3,2,1,0:T(8,128)(2,1)S(1)} %get-tuple-element.12.vf, ...), custom_call_target="tpu_custom_call" | custom-call | tf_op jit(solution)/shard_map/pallas_call | solution.py:394
Async XLA Ops:
  2.5 0.7 copy-start

commit v3 on v2

--- a/solution.py
+++ b/solution.py
@@ -19,7 +19,6 @@
 BF16 = jnp.bfloat16
 ANY = pl.BlockSpec(memory_space=pl.ANY)
 VMEM = pl.BlockSpec(memory_space=pltpu.VMEM)
-SMEM = pl.BlockSpec(memory_space=pltpu.SMEM)
 
 
 def dot(a, b):
@@ -31,9 +30,9 @@
 
 
 def exchange_kernel(
-    chips, steps, plen_ref, k_ref, v_ref, x_ref, gain_ref, wq_ref, wk_ref, wv_ref, wo_ref, cos_ref, sin_ref,
+    chips, steps, plen_hbm, k_ref, v_ref, x_ref, gain_ref, wq_ref, wk_ref, wv_ref, wo_ref, freq_ref,
     kf, vf, kn, vn, yf,
-    stage, gs, hp, wb, sc, pn, xs, wo_own, wo_peer, qs, o_peer, rs,
+    plen_ref, freq, stage, gs, hp, wb, sc, pn, xs, wo_own, wo_peer, qs, o_peer, rs,
     kv_send, kv_recv, kv_own, w_sem, in_sem, wo_sems, o_send, o_recv, rs_send, rs_recv, ag_send, ag_recv, d_send, d_recv,
 ):
     rows, heads, _, head_dim = kn.shape
@@ -99,8 +98,8 @@
 
     loads = [
         pltpu.make_async_copy(gain_ref, gs, in_sem.at[0]),
-        pltpu.make_async_copy(cos_ref, sc.at[:, :rows * head_dim], in_sem.at[1]),
-        pltpu.make_async_copy(sin_ref, sc.at[:, rows * head_dim:2 * rows * head_dim], in_sem.at[2]),
+        pltpu.make_async_copy(freq_ref, freq, in_sem.at[1]),
+        pltpu.make_async_copy(plen_hbm, plen_ref, in_sem.at[2]),
     ]
     for c in loads:
         c.start()
@@ -135,6 +134,12 @@
     def lane_tile(n):
         return pl.ds(pl.multiple_of(n * head_dim, head_dim), head_dim)
 
+    step_id = lax.broadcasted_iota(jnp.int32, (steps, head_dim), 0)
+    for b in range(rows):
+        angles = (step_id + plen_ref[b]).astype(F32) * freq[0:1, :]
+        sc[:, b * head_dim:(b + 1) * head_dim] = jnp.cos(angles)
+        sc[:, (rows + b) * head_dim:(rows + b + 1) * head_dim] = jnp.sin(angles) * freq[1:2, :]
+
     for i, load in enumerate(w_loads):
         load.wait()
         matrix, j = i // groups, i % groups
@@ -279,7 +284,7 @@
                 cache_copy(kind, b, n).wait_send()
 
 
-def write_kernel(plen_ref, kf, vf, kn, vn, yf, k_out, v_out, y_out, win, ys, big_sem, win_sem, y_sem):
+def write_kernel(plen_hbm, kf, vf, kn, vn, yf, k_out, v_out, y_out, plen_ref, win, ys, big_sem, win_sem, y_sem, plen_sem):
     rows, heads, steps, head_dim = kn.shape
     out_len = kf.shape[2]
     span = win.shape[3]
@@ -299,10 +304,13 @@
     for b in range(rows):
         for kind in range(2):
             big(kind, b).start()
+    plen_copy = pltpu.make_async_copy(plen_hbm, plen_ref, plen_sem)
+    plen_copy.start()
     for b in range(rows):
         ys[:, b, :] = yf[b]
     y_copy = pltpu.make_async_copy(ys, y_out, y_sem)
     y_copy.start()
+    plen_copy.wait()
     row_id = lax.broadcasted_iota(jnp.int32, (span, steps), 0)
     col_id = lax.broadcasted_iota(jnp.int32, (span, steps), 1)
     pos = lax.broadcasted_iota(jnp.int32, (span, head_dim), 0)
@@ -344,10 +352,10 @@
         half_dim = head_dim // 2
         inv_freq = (ROPE_BASE ** (-2.0 * np.arange(half_dim) / head_dim)).astype(np.float32)
         sign = np.where(np.arange(head_dim) < half_dim, -1.0, 1.0).astype(np.float32)
-        starts = jnp.broadcast_to(prompt_len[:, None], (rows, head_dim)).reshape(1, rows * head_dim)
-        angles = (jnp.arange(steps)[:, None] + starts).astype(F32) * np.tile(inv_freq, 2 * rows)
-        cos, sin = jnp.cos(angles), jnp.sin(angles) * np.tile(sign, rows)
+        freq = np.zeros((8, head_dim), np.float32)
+        freq[0], freq[1] = np.tile(inv_freq, 2), sign
         dma = pltpu.SemaphoreType.DMA
+        plen = pltpu.with_memory_space_constraint(prompt_len, pltpu.HBM)
         peers = parts - 1
         kf, vf, kn, vn, yf = pl.pallas_call(
             functools.partial(exchange_kernel, chips, steps),
@@ -358,9 +366,11 @@
                 pltpu.VMEM((rows, heads, steps, head_dim), BF16),
                 pltpu.VMEM((rows, steps, model), BF16),
             ),
-            in_specs=[SMEM] + [ANY] * 10,
+            in_specs=[ANY] * 10,
             out_specs=(VMEM,) * 5,
             scratch_shapes=[
+                pltpu.SMEM((rows,), jnp.int32),
+                pltpu.VMEM((8, head_dim), F32),
                 pltpu.VMEM((STAGE_STEPS, rows, model), BF16),
                 pltpu.VMEM((model,), BF16),
                 pltpu.VMEM((max(rows, heads) * steps, max(model, seq_len)), BF16),
@@ -389,7 +399,7 @@
                 dma((rows,)),
             ],
             compiler_params=pltpu.CompilerParams(collective_id=0, has_side_effects=True, vmem_limit_bytes=VMEM_LIMIT),
-        )(prompt_len, *(pltpu.with_memory_space_constraint(a, pltpu.HBM) for a in (k_cache, v_cache, x_steps, w_norm, w_q, w_k, w_v, w_o)), cos, sin)
+        )(plen, *(pltpu.with_memory_space_constraint(a, pltpu.HBM) for a in (k_cache, v_cache, x_steps, w_norm, w_q, w_k, w_v, w_o, jnp.asarray(freq))))
         span = steps + WINDOW_ALIGN
         k_out, v_out, y = pl.pallas_call(
             write_kernel,
@@ -398,17 +408,19 @@
                 jax.ShapeDtypeStruct((rows, heads, out_len, head_dim), BF16),
                 jax.ShapeDtypeStruct((steps, rows, model), BF16),
             ),
-            in_specs=[SMEM] + [VMEM] * 5,
+            in_specs=[ANY] + [VMEM] * 5,
             out_specs=(ANY,) * 3,
             scratch_shapes=[
+                pltpu.SMEM((rows,), jnp.int32),
                 pltpu.VMEM((2, rows, heads, span, head_dim), BF16),
                 pltpu.VMEM((steps, rows, model), BF16),
                 dma((2, rows)),
                 dma((2, rows)),
                 dma,
+                dma,
             ],
             compiler_params=pltpu.CompilerParams(vmem_limit_bytes=6 << 20),
-        )(prompt_len, kf, vf, kn, vn, yf)
+        )(plen, kf, vf, kn, vn, yf)
         return y, k_out, v_out
 
     cache_spec = P("dp", None, "tp", None)

time: 409 us -> 406 us (level)
  no operation moved by 1% of the time
where the time goes in v3:
time: 406 us
  Pallas kernels  405 us (100%)
    pallas_call x1, Pallas kernels, local_block(): pl.pallas_call(functools.partial(exchange_kernel, chips, steps), out_shap...  393 us
    pallas_call x1, Pallas kernels, local_block(): pl.pallas_call(write_kernel, out_shape=(jax.ShapeDtypeStruct((rows, heads...  12 us

profile of v3, /device:TPU:113, one launch (start us, length us, event | category | flops | bytes accessed | tf_op | source)
XLA Modules:
  0.0 405.6 jit_solution(14579399150061444330)
XLA Ops:
  0.6 392.8 %shard_map.121 = (bf16[4,4,4160,128]{3,2,1,0:T(8,128)(2,1)S(1)}, bf16[4,4,4160,128]{3,2,1,0:T(8,128)(2,1)S(1)}, bf16[4,4,64,128]{3,2,1,0:T(8,128)(2,1)S(1)}, bf1...) custom-call(s32[4]{0:T(128)} %plen_hbm.3, bf16[4,32,512,128]{3,2,1,0:T(8,128)(2,1)} %k_ref.1, ...), custom_call_target="tpu_custom_call" | custom-call | tf_op jit(solution)/shard_map/pallas_call | solution.py:360
  393.4 12.0 %shard_map.122 = (bf16[4,4,4160,128]{3,2,1,0:T(8,128)(2,1)}, bf16[4,4,4160,128]{3,2,1,0:T(8,128)(2,1)}, bf16[64,4,4096]{2,1,0:T(4,128)(2,1)}) custom-call(s32[4]{0:T(128)} %plen_hbm.3, bf16[4,4,4160,128]{3,2,1,0:T(8,128)(2,1)S(1)} %get-tuple-element.11.kf, bf16[4,4,4160,128]{3,2,1,0:T(8,128)(2,1)S(1)} %get-tuple-element.12.vf, ...), custom_call_target="tpu_custom_call" | custom-call | tf_op jit(solution)/shard_map/pallas_call | solution.py:404

commit v4 on v3

--- a/solution.py
+++ b/solution.py
@@ -33,7 +33,7 @@
     chips, steps, plen_hbm, k_ref, v_ref, x_ref, gain_ref, wq_ref, wk_ref, wv_ref, wo_ref, freq_ref,
     kf, vf, kn, vn, yf,
     plen_ref, freq, stage, gs, hp, wb, sc, pn, xs, wo_own, wo_peer, qs, o_peer, rs,
-    kv_send, kv_recv, kv_own, w_sem, in_sem, wo_sems, o_send, o_recv, rs_send, rs_recv, ag_send, ag_recv, d_send, d_recv,
+    kv_send, kv_recv, kv_own, w_sem, in_sem, wo_sems, o_send, o_recv, rs_send, rs_recv, ag_send, ag_recv, fw_send, fw_recv, d_send, d_recv,
 ):
     rows, heads, _, head_dim = kn.shape
     out_len = kf.shape[2]
@@ -248,10 +248,19 @@
         for d in range(1, chips):
             rs_copy(b, d).start()
 
-    def ag_copy(b, d):
-        to = lax.rem(chip + d, chips)
+    sides = (1, chips - 1)
+
+    def ag_copy(b, side):
         mine = yf.at[b, :, columns(core, chip)]
-        return remote(mine, mine, ag_send.at[b, d - 1], ag_recv.at[b, d - 1], to * CORES + core)
+        to = lax.rem(chip + sides[side], chips)
+        return remote(mine, mine, ag_send.at[b, side], ag_recv.at[b, side], to * CORES + core)
+
+    def pass_copy(b, side):
+        owner = lax.rem(chip + sides[1 - side], chips)
+        part = block // 2
+        cols = pl.ds(pl.multiple_of(core * half + owner * block + side * part, part), part)
+        to = lax.rem(chip + sides[side], chips)
+        return remote(yf.at[b, :, cols], yf.at[b, :, cols], fw_send.at[b, side], fw_recv.at[b, side], to * CORES + core)
 
     def d_copy(b):
         mine = yf.at[b, :, half_cols(core)]
@@ -267,18 +276,24 @@
                 attn = attn + rs[b, d - 1, tile * steps:(tile + 1) * steps].astype(F32)
             out_cols = pl.ds(pl.multiple_of(core * half + chip * block + tile * lanes, lanes), lanes)
             yf[b, :, out_cols] = (xs[b, :, cols].astype(F32) + attn).astype(BF16)
-        for d in range(1, chips):
-            ag_copy(b, d).start()
-    for b in range(rows):
-        for d in range(1, chips):
-            ag_copy(b, d).wait_recv()
+        for side in range(2):
+            ag_copy(b, side).start()
+    for b in range(rows):
+        for side in range(2):
+            ag_copy(b, side).wait_recv()
+            pass_copy(b, side).start()
+    for b in range(rows):
+        for side in range(2):
+            pass_copy(b, side).wait_recv()
         d_copy(b).start()
     for b in range(rows):
         d_copy(b).wait()
         o_copy(b).wait_send()
         for d in range(1, chips):
             rs_copy(b, d).wait_send()
-            ag_copy(b, d).wait_send()
+        for side in range(2):
+            ag_copy(b, side).wait_send()
+            pass_copy(b, side).wait_send()
         for kind in range(2):
             for n in range(len(hops)):
                 cache_copy(kind, b, n).wait_send()
@@ -338,6 +353,7 @@
 def solution(mesh):
     parts = mesh.shape["tp"]
     chips = parts // CORES
+    assert chips == 4
 
     def local_block(k_cache, v_cache, prompt_len, x_steps, w_norm, w_q, w_k, w_v, w_o):
         rows, _, shard, head_dim = k_cache.shape
@@ -393,8 +409,10 @@
                 dma((rows,)),
                 dma((rows, chips - 1)),
                 dma((rows, chips - 1)),
-                dma((rows, chips - 1)),
-                dma((rows, chips - 1)),
+                dma((rows, 2)),
+                dma((rows, 2)),
+                dma((rows, 2)),
+                dma((rows, 2)),
                 dma((rows,)),
                 dma((rows,)),
             ],

time: 406 us -> 403 us (level)
  no operation moved by 1% of the time
where the time goes in v4:
time: 403 us
  Pallas kernels  402 us (100%)
    pallas_call x1, Pallas kernels, local_block(): pl.pallas_call(functools.partial(exchange_kernel, chips, steps), out_shap...  390 us
    pallas_call x1, Pallas kernels, local_block(): pl.pallas_call(write_kernel, out_shape=(jax.ShapeDtypeStruct((rows, heads...  12 us

profile of v4, /device:TPU:113, one launch (start us, length us, event | category | flops | bytes accessed | tf_op | source)
XLA Modules:
  0.0 403.0 jit_solution(9397527243732494717)
XLA Ops:
  0.6 390.3 %shard_map.121 = (bf16[4,4,4160,128]{3,2,1,0:T(8,128)(2,1)S(1)}, bf16[4,4,4160,128]{3,2,1,0:T(8,128)(2,1)S(1)}, bf16[4,4,64,128]{3,2,1,0:T(8,128)(2,1)S(1)}, bf1...) custom-call(s32[4]{0:T(128)} %plen_hbm.3, bf16[4,32,512,128]{3,2,1,0:T(8,128)(2,1)} %k_ref.1, ...), custom_call_target="tpu_custom_call" | custom-call | tf_op jit(solution)/shard_map/pallas_call | solution.py:376
  390.9 12.0 %shard_map.122 = (bf16[4,4,4160,128]{3,2,1,0:T(8,128)(2,1)}, bf16[4,4,4160,128]{3,2,1,0:T(8,128)(2,1)}, bf16[64,4,4096]{2,1,0:T(4,128)(2,1)}) custom-call(s32[4]{0:T(128)} %plen_hbm.3, bf16[4,4,4160,128]{3,2,1,0:T(8,128)(2,1)S(1)} %get-tuple-element.11.kf, bf16[4,4,4160,128]{3,2,1,0:T(8,128)(2,1)S(1)} %get-tuple-element.12.vf, ...), custom_call_target="tpu_custom_call" | custom-call | tf_op jit(solution)/shard_map/pallas_call | solution.py:422

commit v5 on v4

--- a/solution.py
+++ b/solution.py
@@ -255,16 +255,24 @@
         to = lax.rem(chip + sides[side], chips)
         return remote(mine, mine, ag_send.at[b, side], ag_recv.at[b, side], to * CORES + core)
 
-    def pass_copy(b, side):
+    def pass_copy(b, side, flip=0):
         owner = lax.rem(chip + sides[1 - side], chips)
         part = block // 2
         cols = pl.ds(pl.multiple_of(core * half + owner * block + side * part, part), part)
         to = lax.rem(chip + sides[side], chips)
-        return remote(yf.at[b, :, cols], yf.at[b, :, cols], fw_send.at[b, side], fw_recv.at[b, side], to * CORES + core)
+        n = b + flip
+        target = to * CORES + lax.rem(core + flip, CORES)
+        return remote(yf.at[b, :, cols], yf.at[b, :, cols], fw_send.at[n, side], fw_recv.at[n, side], target)
 
     def d_copy(b):
         mine = yf.at[b, :, half_cols(core)]
         return remote(mine, mine, d_send.at[b], d_recv.at[b], partner)
+
+    last = rows - 1
+
+    def d_block(n):
+        mine = yf.at[last, :, columns(core, lax.rem(chip + (0, chips - 1, 1)[n], chips))]
+        return remote(mine, mine, d_send.at[last + n], d_recv.at[last + n], partner)
 
     for b in range(rows):
         for d in range(1, chips):
@@ -278,22 +286,33 @@
             yf[b, :, out_cols] = (xs[b, :, cols].astype(F32) + attn).astype(BF16)
         for side in range(2):
             ag_copy(b, side).start()
+    d_block(0).start()
     for b in range(rows):
         for side in range(2):
             ag_copy(b, side).wait_recv()
             pass_copy(b, side).start()
-    for b in range(rows):
+            if b == last:
+                pass_copy(b, side, 1).start()
+                d_block(1 + side).start()
+    for b in range(last):
         for side in range(2):
             pass_copy(b, side).wait_recv()
         d_copy(b).start()
-    for b in range(rows):
+    for b in range(last):
         d_copy(b).wait()
+    for n in range(3):
+        d_block(n).wait()
+    for side in range(2):
+        for flip in range(2):
+            pass_copy(last, side, flip).wait()
+    for b in range(rows):
         o_copy(b).wait_send()
         for d in range(1, chips):
             rs_copy(b, d).wait_send()
         for side in range(2):
             ag_copy(b, side).wait_send()
-            pass_copy(b, side).wait_send()
+            if b < last:
+                pass_copy(b, side).wait_send()
         for kind in range(2):
             for n in range(len(hops)):
                 cache_copy(kind, b, n).wait_send()
@@ -309,16 +328,21 @@
         p = plen_ref[b]
         return pl.multiple_of(jnp.minimum(p - lax.rem(p, WINDOW_ALIGN), last), WINDOW_ALIGN)
 
-    def big(kind, b):
+    lower = (out_len - steps) // 2
+
+    def big(kind, b, upper):
         src, dst = ((kf, k_out), (vf, v_out))[kind]
-        return pltpu.make_async_copy(src.at[b], dst.at[b], big_sem.at[kind, b])
+        part = slice(lower, out_len) if upper else slice(0, lower)
+        return pltpu.make_async_copy(src.at[b, :, part], dst.at[b, :, part], big_sem.at[upper, kind, b])
 
     def small(kind, b):
         return pltpu.make_async_copy(win.at[kind, b], (k_out, v_out)[kind].at[b, :, pl.ds(start_of(b), span), :], win_sem.at[kind, b])
 
     for b in range(rows):
         for kind in range(2):
-            big(kind, b).start()
+            big(kind, b, 1).start()
+    for kind in range(2):
+        big(kind, 0, 0).start()
     plen_copy = pltpu.make_async_copy(plen_hbm, plen_ref, plen_sem)
     plen_copy.start()
     for b in range(rows):
@@ -342,11 +366,14 @@
                 win[kind, b, h] = jnp.where(fresh, moved, kept).astype(BF16)
     for b in range(rows):
         for kind in range(2):
-            big(kind, b).wait()
+            big(kind, b, 1).wait()
             small(kind, b).start()
+            if b + 1 < rows:
+                big(kind, b + 1, 0).start()
     y_copy.wait()
     for b in range(rows):
         for kind in range(2):
+            big(kind, b, 0).wait()
             small(kind, b).wait()
 
 
@@ -411,10 +438,10 @@
                 dma((rows, chips - 1)),
                 dma((rows, 2)),
                 dma((rows, 2)),
-                dma((rows, 2)),
-                dma((rows, 2)),
-                dma((rows,)),
-                dma((rows,)),
+                dma((rows + 1, 2)),
+                dma((rows + 1, 2)),
+                dma((rows + 2,)),
+                dma((rows + 2,)),
             ],
             compiler_params=pltpu.CompilerParams(collective_id=0, has_side_effects=True, vmem_limit_bytes=VMEM_LIMIT),
         )(plen, *(pltpu.with_memory_space_constraint(a, pltpu.HBM) for a in (k_cache, v_cache, x_steps, w_norm, w_q, w_k, w_v, w_o, jnp.asarray(freq))))
@@ -432,7 +459,7 @@
                 pltpu.SMEM((rows,), jnp.int32),
                 pltpu.VMEM((2, rows, heads, span, head_dim), BF16),
                 pltpu.VMEM((steps, rows, model), BF16),
-                dma((2, rows)),
+                dma((2, 2, rows)),
                 dma((2, rows)),
                 dma,
                 dma,

time: 403 us -> 403 us (level)
  no operation moved by 1% of the time
where the time goes in v5:
time: 403 us; the launch traced here: 402 us
  Pallas kernels  401 us (100%)
    pallas_call x1, Pallas kernels, local_block(): pl.pallas_call(functools.partial(exchange_kernel, chips, steps), out_shap...  389 us
    pallas_call x1, Pallas kernels, local_block(): pl.pallas_call(write_kernel, out_shape=(jax.ShapeDtypeStruct((rows, heads...  12.1 us

profile of v5, /device:TPU:113, one launch (start us, length us, event | category | flops | bytes accessed | tf_op | source)
XLA Modules:
  0.0 402.3 jit_solution(10609361454072489511)
XLA Ops:
  0.6 389.4 %shard_map.121 = (bf16[4,4,4160,128]{3,2,1,0:T(8,128)(2,1)S(1)}, bf16[4,4,4160,128]{3,2,1,0:T(8,128)(2,1)S(1)}, bf16[4,4,64,128]{3,2,1,0:T(8,128)(2,1)S(1)}, bf1...) custom-call(s32[4]{0:T(128)} %plen_hbm.3, bf16[4,32,512,128]{3,2,1,0:T(8,128)(2,1)} %k_ref.1, ...), custom_call_target="tpu_custom_call" | custom-call | tf_op jit(solution)/shard_map/pallas_call | solution.py:403
  390.0 12.1 %shard_map.122 = (bf16[4,4,4160,128]{3,2,1,0:T(8,128)(2,1)}, bf16[4,4,4160,128]{3,2,1,0:T(8,128)(2,1)}, bf16[64,4,4096]{2,1,0:T(4,128)(2,1)}) custom-call(s32[4]{0:T(128)} %plen_hbm.3, bf16[4,4,4160,128]{3,2,1,0:T(8,128)(2,1)S(1)} %get-tuple-element.11.kf, bf16[4,4,4160,128]{3,2,1,0:T(8,128)(2,1)S(1)} %get-tuple-element.12.vf, ...), custom_call_target="tpu_custom_call" | custom-call | tf_op jit(solution)/shard_map/pallas_call | solution.py:449

commit v6 on v5

--- a/solution.py
+++ b/solution.py
@@ -33,7 +33,7 @@
     chips, steps, plen_hbm, k_ref, v_ref, x_ref, gain_ref, wq_ref, wk_ref, wv_ref, wo_ref, freq_ref,
     kf, vf, kn, vn, yf,
     plen_ref, freq, stage, gs, hp, wb, sc, pn, xs, wo_own, wo_peer, qs, o_peer, rs,
-    kv_send, kv_recv, kv_own, w_sem, in_sem, wo_sems, o_send, o_recv, rs_send, rs_recv, ag_send, ag_recv, fw_send, fw_recv, d_send, d_recv,
+    kv_send, kv_recv, kv_own, first_send, w_sem, in_sem, wo_sems, o_send, o_recv, rs_send, rs_recv, ag_send, ag_recv, fw_send, fw_recv, d_send, d_recv,
 ):
     rows, heads, _, head_dim = kn.shape
     out_len = kf.shape[2]
@@ -58,6 +58,12 @@
     def remote(src, dst, send, recv, target):
         return pltpu.make_async_remote_copy(src_ref=src, dst_ref=dst, send_sem=send, recv_sem=recv, device_id=(group, target), device_id_type=MESH)
 
+    def first_load(n):
+        return pltpu.make_async_copy(k_ref.at[0, pl.ds(peer(hops[n]) * heads, heads), :steps], qs.at[n], in_sem.at[5 + n])
+
+    for n in range(2):
+        first_load(n).start()
+
     barrier = pltpu.get_barrier_semaphore()
     for hop in hops:
         pl.semaphore_signal(barrier, inc=1, device_id=(group, peer(hop)), device_id_type=MESH)
@@ -68,7 +74,18 @@
     def cache_copy(kind, b, n):
         src, dst = ((k_ref, kf), (v_ref, vf))[kind]
         target = peer(hops[n])
-        return remote(src.at[b, pl.ds(target * heads, heads)], dst.at[b, :, slots, :], kv_send.at[kind, b, n], kv_recv.at[kind, b, n], target)
+        skip = steps if kind == 0 and isinstance(b, int) and b == 0 and n < 2 else 0
+        return remote(
+            src.at[b, pl.ds(target * heads, heads), skip:],
+            dst.at[b, :, pl.ds(pl.multiple_of(me * shard + skip, WINDOW_ALIGN), shard - skip), :],
+            kv_send.at[kind, b, n],
+            kv_recv.at[kind, b, n],
+            target,
+        )
+
+    def first_copy(n):
+        dst = kf.at[0, :, pl.ds(pl.multiple_of(me * shard, shard), steps), :]
+        return remote(qs.at[n], dst, first_send.at[n], kv_recv.at[0, 0, n], peer(hops[n]))
 
     def own_copy(kind, b):
         src, dst = ((k_ref, kf), (v_ref, vf))[kind]
@@ -78,10 +95,15 @@
         return pl.ds(pl.multiple_of(which * half, half), half)
 
     wo_send = remote(wo_ref.at[:, half_cols(1 - core)], wo_peer, wo_sems.at[0], wo_sems.at[1], partner)
+    for n in range(2):
+        first_load(n).wait()
+        first_copy(n).start()
+    for n in range(2):
+        cache_copy(0, 0, n).start()
     wo_send.start()
     for b in range(rows):
         for kind in range(2):
-            for n in range(len(hops)):
+            for n in range(2 if b == kind == 0 else 0, len(hops)):
                 cache_copy(kind, b, n).start()
 
     for b in range(rows):
@@ -140,6 +162,8 @@
         sc[:, b * head_dim:(b + 1) * head_dim] = jnp.cos(angles)
         sc[:, (rows + b) * head_dim:(rows + b + 1) * head_dim] = jnp.sin(angles) * freq[1:2, :]
 
+    for n in range(2):
+        first_copy(n).wait_send()
     for i, load in enumerate(w_loads):
         load.wait()
         matrix, j = i // groups, i % groups
@@ -429,8 +453,9 @@
                 dma((2, rows, peers)),
                 dma((2, rows, peers)),
                 dma((2, rows)),
+                dma((2,)),
                 dma((3 * width // head_dim,)),
-                dma((5,)),
+                dma((7,)),
                 dma((2,)),
                 dma((rows,)),
                 dma((rows,)),

time: 403 us -> 403 us (level)
  no operation moved by 1% of the time
where the time goes in v6:
time: 403 us; the launch traced here: 402 us
  Pallas kernels  402 us (100%)
    pallas_call x1, Pallas kernels, local_block(): pl.pallas_call(functools.partial(exchange_kernel, chips, steps), out_shap...  389 us
    pallas_call x1, Pallas kernels, local_block(): pl.pallas_call(write_kernel, out_shape=(jax.ShapeDtypeStruct((rows, heads...  12.1 us

profile of v6, /device:TPU:113, one launch (start us, length us, event | category | flops | bytes accessed | tf_op | source)
XLA Modules:
  0.0 402.3 jit_solution(5064579296103173067)
XLA Ops:
  0.6 389.4 %shard_map.121 = (bf16[4,4,4160,128]{3,2,1,0:T(8,128)(2,1)S(1)}, bf16[4,4,4160,128]{3,2,1,0:T(8,128)(2,1)S(1)}, bf16[4,4,64,128]{3,2,1,0:T(8,128)(2,1)S(1)}, bf1...) custom-call(s32[4]{0:T(128)} %plen_hbm.3, bf16[4,32,512,128]{3,2,1,0:T(8,128)(2,1)} %k_ref.1, ...), custom_call_target="tpu_custom_call" | custom-call | tf_op jit(solution)/shard_map/pallas_call | solution.py:427
  390.1 12.1 %shard_map.122 = (bf16[4,4,4160,128]{3,2,1,0:T(8,128)(2,1)}, bf16[4,4,4160,128]{3,2,1,0:T(8,128)(2,1)}, bf16[64,4,4096]{2,1,0:T(4,128)(2,1)}) custom-call(s32[4]{0:T(128)} %plen_hbm.3, bf16[4,4,4160,128]{3,2,1,0:T(8,128)(2,1)S(1)} %get-tuple-element.11.kf, bf16[4,4,4160,128]{3,2,1,0:T(8,128)(2,1)S(1)} %get-tuple-element.12.vf, ...), custom_call_target="tpu_custom_call" | custom-call | tf_op jit(solution)/shard_map/pallas_call | solution.py:474

commit v7 on v5

--- a/solution.py
+++ b/solution.py
@@ -328,21 +328,17 @@
         p = plen_ref[b]
         return pl.multiple_of(jnp.minimum(p - lax.rem(p, WINDOW_ALIGN), last), WINDOW_ALIGN)
 
-    lower = (out_len - steps) // 2
-
-    def big(kind, b, upper):
+    def big(kind, b, h):
         src, dst = ((kf, k_out), (vf, v_out))[kind]
-        part = slice(lower, out_len) if upper else slice(0, lower)
-        return pltpu.make_async_copy(src.at[b, :, part], dst.at[b, :, part], big_sem.at[upper, kind, b])
+        return pltpu.make_async_copy(src.at[b, h], dst.at[b, h], big_sem.at[kind, b, h])
 
     def small(kind, b):
         return pltpu.make_async_copy(win.at[kind, b], (k_out, v_out)[kind].at[b, :, pl.ds(start_of(b), span), :], win_sem.at[kind, b])
 
     for b in range(rows):
         for kind in range(2):
-            big(kind, b, 1).start()
-    for kind in range(2):
-        big(kind, 0, 0).start()
+            for h in range(heads):
+                big(kind, b, h).start()
     plen_copy = pltpu.make_async_copy(plen_hbm, plen_ref, plen_sem)
     plen_copy.start()
     for b in range(rows):
@@ -366,14 +362,12 @@
                 win[kind, b, h] = jnp.where(fresh, moved, kept).astype(BF16)
     for b in range(rows):
         for kind in range(2):
-            big(kind, b, 1).wait()
+            for h in range(heads):
+                big(kind, b, h).wait()
             small(kind, b).start()
-            if b + 1 < rows:
-                big(kind, b + 1, 0).start()
     y_copy.wait()
     for b in range(rows):
         for kind in range(2):
-            big(kind, b, 0).wait()
             small(kind, b).wait()
 
 
@@ -459,7 +453,7 @@
                 pltpu.SMEM((rows,), jnp.int32),
                 pltpu.VMEM((2, rows, heads, span, head_dim), BF16),
                 pltpu.VMEM((steps, rows, model), BF16),
-                dma((2, 2, rows)),
+                dma((2, rows, heads)),
                 dma((2, rows)),
                 dma,
                 dma,

time: 403 us -> 403 us (level)
  no operation moved by 1% of the time
where the time goes in v7:
time: 403 us; the launch traced here: 402 us
  Pallas kernels  402 us (100%)
    pallas_call x1, Pallas kernels, local_block(): pl.pallas_call(functools.partial(exchange_kernel, chips, steps), out_shap...  389 us
    pallas_call x1, Pallas kernels, local_block(): pl.pallas_call(write_kernel, out_shape=(jax.ShapeDtypeStruct((rows, heads...  12.2 us

profile of v7, /device:TPU:113, one launch (start us, length us, event | category | flops | bytes accessed | tf_op | source)
XLA Modules:
  0.0 402.4 jit_solution(4297749740565257388)
XLA Ops:
  0.6 389.4 %shard_map.121 = (bf16[4,4,4160,128]{3,2,1,0:T(8,128)(2,1)S(1)}, bf16[4,4,4160,128]{3,2,1,0:T(8,128)(2,1)S(1)}, bf16[4,4,64,128]{3,2,1,0:T(8,128)(2,1)S(1)}, bf1...) custom-call(s32[4]{0:T(128)} %plen_hbm.3, bf16[4,32,512,128]{3,2,1,0:T(8,128)(2,1)} %k_ref.1, ...), custom_call_target="tpu_custom_call" | custom-call | tf_op jit(solution)/shard_map/pallas_call | solution.py:397
  390.0 12.2 %shard_map.122 = (bf16[4,4,4160,128]{3,2,1,0:T(8,128)(2,1)}, bf16[4,4,4160,128]{3,2,1,0:T(8,128)(2,1)}, bf16[64,4,4096]{2,1,0:T(4,128)(2,1)}) custom-call(s32[4]{0:T(128)} %plen_hbm.3, bf16[4,4,4160,128]{3,2,1,0:T(8,128)(2,1)S(1)} %get-tuple-element.11.kf, bf16[4,4,4160,128]{3,2,1,0:T(8,128)(2,1)S(1)} %get-tuple-element.12.vf, ...), custom_call_target="tpu_custom_call" | custom-call | tf_op jit(solution)/shard_map/pallas_call | solution.py:443

commit v8 on v7

--- a/solution.py
+++ b/solution.py
@@ -328,17 +328,16 @@
         p = plen_ref[b]
         return pl.multiple_of(jnp.minimum(p - lax.rem(p, WINDOW_ALIGN), last), WINDOW_ALIGN)
 
-    def big(kind, b, h):
+    def big(kind, b):
         src, dst = ((kf, k_out), (vf, v_out))[kind]
-        return pltpu.make_async_copy(src.at[b, h], dst.at[b, h], big_sem.at[kind, b, h])
+        return pltpu.make_async_copy(src.at[b], dst.at[b], big_sem.at[kind, b])
 
     def small(kind, b):
         return pltpu.make_async_copy(win.at[kind, b], (k_out, v_out)[kind].at[b, :, pl.ds(start_of(b), span), :], win_sem.at[kind, b])
 
     for b in range(rows):
         for kind in range(2):
-            for h in range(heads):
-                big(kind, b, h).start()
+            big(kind, b).start()
     plen_copy = pltpu.make_async_copy(plen_hbm, plen_ref, plen_sem)
     plen_copy.start()
     for b in range(rows):
@@ -362,8 +361,7 @@
                 win[kind, b, h] = jnp.where(fresh, moved, kept).astype(BF16)
     for b in range(rows):
         for kind in range(2):
-            for h in range(heads):
-                big(kind, b, h).wait()
+            big(kind, b).wait()
             small(kind, b).start()
     y_copy.wait()
     for b in range(rows):
@@ -453,7 +451,7 @@
                 pltpu.SMEM((rows,), jnp.int32),
                 pltpu.VMEM((2, rows, heads, span, head_dim), BF16),
                 pltpu.VMEM((steps, rows, model), BF16),
-                dma((2, rows, heads)),
+                dma((2, rows)),
                 dma((2, rows)),
                 dma,
                 dma,

time: 403 us -> 402 us (level)
  no operation moved by 1% of the time
where the time goes in v8:
time: 402 us
  Pallas kernels  401 us (100%)
    pallas_call x1, Pallas kernels, local_block(): pl.pallas_call(functools.partial(exchange_kernel, chips, steps), out_shap...  389 us
    pallas_call x1, Pallas kernels, local_block(): pl.pallas_call(write_kernel, out_shape=(jax.ShapeDtypeStruct((rows, heads...  12 us

profile of v8, /device:TPU:113, one launch (start us, length us, event | category | flops | bytes accessed | tf_op | source)
XLA Modules:
  0.0 402.2 jit_solution(14028734340826342851)
XLA Ops:
  0.6 389.4 %shard_map.121 = (bf16[4,4,4160,128]{3,2,1,0:T(8,128)(2,1)S(1)}, bf16[4,4,4160,128]{3,2,1,0:T(8,128)(2,1)S(1)}, bf16[4,4,64,128]{3,2,1,0:T(8,128)(2,1)S(1)}, bf1...) custom-call(s32[4]{0:T(128)} %plen_hbm.3, bf16[4,32,512,128]{3,2,1,0:T(8,128)(2,1)} %k_ref.1, ...), custom_call_target="tpu_custom_call" | custom-call | tf_op jit(solution)/shard_map/pallas_call | solution.py:395
  390.0 12.0 %shard_map.122 = (bf16[4,4,4160,128]{3,2,1,0:T(8,128)(2,1)}, bf16[4,4,4160,128]{3,2,1,0:T(8,128)(2,1)}, bf16[64,4,4096]{2,1,0:T(4,128)(2,1)}) custom-call(s32[4]{0:T(128)} %plen_hbm.3, bf16[4,4,4160,128]{3,2,1,0:T(8,128)(2,1)S(1)} %get-tuple-element.11.kf, bf16[4,4,4160,128]{3,2,1,0:T(8,128)(2,1)S(1)} %get-tuple-element.12.vf, ...), custom_call_target="tpu_custom_call" | custom-call | tf_op jit(solution)/shard_map/pallas_call | solution.py:441
